TPU v7x, 512 devices: a whole 4x8x8 slice. The times are simulated.
512 devices in a mesh: dp: 128 (over z, y, core), mp: 4 (over x).
Axes of the slice: x: 4, y: 8, z: 8, core: 2. Of those that a mesh axis runs over, the one named last changes fastest.
Arguments:
- tokens: bfloat16 [32768, 4096], P('dp', 'mp'), may hold values from -6 to 6
- router_weight: bfloat16 [4096, 64], P('mp'), may hold values from -1 to 1
- valid_count: int32 [128], P('dp'), may hold values from 64 to 256, as said below
- expert_id: int32 [32768], P('dp'), may hold values from 0 to 63, as said below
- slot_id: int32 [32768], P('dp'), may hold values from 0 to 5
Outputs:
- gates: float32 [32768], P('dp')
- dispatched: bfloat16 [384, 128, 4096], P('dp', None, 'mp')
Inputs may be any that keep to these rules, and one draw needn't show every extreme that they name: Group g's live tokens are its first valid_count[g] positions; the last group is full. Within one group no two positions share an expert and a slot. Flat slots expert_id * 6 + slot_id are held 3 in a row by one owner; one group's positions take at most 2 slots of any owner, and in every group some owner has 2 of its slots taken by live tokens.
All inputs are finite; a program needn't handle non-finite values.
Results may differ from a plain program's by a relative error of at most 0.001.
Values may be sent and summed in bfloat16 or wider, within the bound.
A program may use at most 64 MiB of HBM per device.

v0:
```python
import jax
import jax.numpy as jnp
from jax import lax
from jax.sharding import Mesh
from jax.sharding import PartitionSpec as P

E = 64
ITERS = 5
CAP = 6
DP = ("dp_0", "dp_1", "dp_2")


def split_up(value, dim, size):
    lengths = value.shape
    pieces = value.reshape(*lengths[:dim], size, lengths[dim] // size, *lengths[dim + 1 :])
    return jnp.moveaxis(pieces, dim, 0)


def joined_along(pieces, dim):
    pieces = jnp.moveaxis(pieces, 0, dim)
    lengths = pieces.shape
    return pieces.reshape(*lengths[:dim], lengths[dim] * lengths[dim + 1], *lengths[dim + 2 :])


def moved_by_axis(pieces, axes, sequence):
    lengths = [lax.axis_size(a) for a in axes]
    pieces = pieces.reshape(*lengths, *pieces.shape[1:])
    for k in sequence:
        pieces = lax.all_to_all(pieces, axes[k], split_axis=k, concat_axis=k, tiled=True)
    return pieces.reshape(-1, *pieces.shape[len(axes) :])


def core_and_chips(value, groups, sequence, split_dim, concat_dim):
    size = lax.axis_size(groups[0]) * lax.axis_size(groups[1])
    pieces = split_up(value, split_dim, size)
    return joined_along(moved_by_axis(pieces, groups, sequence), concat_dim)


def copy_for_each(value, axis):
    size = lax.axis_size(axis)
    return lax.all_to_all(
        jnp.broadcast_to(value[None], (size, *value.shape)), axis, 0, 0, tiled=True
    )


def over_copies(value, axis):
    return copy_for_each(value, axis).sum(axis=0)


def by_axis(value, axes):
    far, near = axes
    nearer = over_copies(value, near)
    return over_copies(nearer, far)


def dispatch(tokens, live, expert_id, slot_id):
    total_slots = E * CAP
    target = expert_id * CAP + slot_id
    placed = jnp.where(live, target, total_slots)
    buffer = (
        jnp.zeros((total_slots, tokens.shape[1]), jnp.bfloat16).at[placed].set(tokens, mode="drop")
    )
    return core_and_chips(buffer[:, None, :], (("dp_0", "dp_1"), "dp_2"), (1, 0), 0, 1)


def balance(logits, live, expert_id, total, column_sum):
    experts = logits.shape[1]
    affinity = jnp.exp(logits)
    weight = live.astype(jnp.float32)
    col_scale = jnp.ones((experts,), jnp.float32)
    row_scale = jnp.ones((logits.shape[0],), jnp.float32)
    for sweep in range(ITERS):
        row_scale = experts / jnp.sum(affinity * col_scale[None, :], axis=1)
        column = column_sum(jnp.sum(affinity * (weight * row_scale)[:, None], axis=0))
        col_scale = total / column
    chosen = expert_id[:, None] == jnp.arange(experts, dtype=jnp.int32)[None, :]
    picked = jnp.sum(jnp.where(chosen, affinity * col_scale[None, :], 0.0), axis=1)
    return weight * row_scale * picked


def local(tokens, router_weight, valid_count, expert_id, slot_id):
    rows = tokens.shape[0]
    live = jnp.arange(rows, dtype=jnp.int32) < valid_count[0]
    dispatched = None
    total = by_axis(valid_count.astype(jnp.float32)[0], (("dp_0", "dp_1"), "dp_2"))
    partial_logits = jnp.dot(tokens, router_weight, preferred_element_type=jnp.float32)
    logits = over_copies(partial_logits, "mp")

    def group_sum(partial_value):
        return by_axis(partial_value, (("dp_0", "dp_1"), "dp_2"))

    gates = balance(logits, live, expert_id, total, group_sum)
    dispatched = dispatch(tokens, live, expert_id, slot_id)
    return (gates, dispatched)


def solution(mesh):
    torus = Mesh(mesh.devices.reshape(8, 8, 2, mesh.shape["mp"]), ("dp_0", "dp_1", "dp_2", "mp"))
    return jax.shard_map(
        local,
        mesh=torus,
        in_specs=(P(DP, "mp"), P("mp", None), P(DP), P(DP), P(DP)),
        out_specs=(P(DP), P(DP, None, "mp")),
        check_vma=False,
    )
```

profile of v0, /device:TPU:8, one launch (start us, length us, event | category | flops | bytes accessed | tf_op | source)
XLA Modules:
  0.0 191.4 jit_solution(8152105678505576566)
XLA Ops:
  1.3 0.6 broadcast_in_dim.40
  1.9 3.2 %all-to-all-start.1 = ((f32[2,1,1]{2,1,0:T(1,128)}), f32[2,1,1]{2,1,0:T(1,128)S(1)}, u32[]{:S(2)}, u32[]{:S(2)}) async-start(f32[2,1,1]{2,1,0:T(1,128)} %broadcast_in_dim.40), calls=%async_computation.1 | async-start | bytes 2048 | tf_op jit(solution)/shard_map/all_to_all | solution.py:41
  5.1 1.3 fusion.2
  6.4 0.7 broadcast_in_dim.38
  7.2 4.3 %all-to-all-start = ((f32[4,256,64]{1,2,0:T(8,128)}), f32[4,256,64]{1,2,0:T(8,128)S(1)}, u32[]{:S(2)}, u32[]{:S(2)}) async-start(f32[4,256,64]{1,2,0:T(8,128)} %broadcast_in_dim.38), calls=%async_computation | async-start | bytes 524288 | tf_op jit(solution)/shard_map/all_to_all | solution.py:41
  11.5 0.6 reduce_sum.217
  12.1 6.7 %all-to-all-done = f32[4,256,64]{1,2,0:T(8,128)S(1)} async-done(((f32[4,256,64]{1,2,0:T(8,128)}), f32[4,256,64]{1,2,0:T(8,128)S(1)}, u32[]{:S(2)}, u32[]{:S(2)}) %all-to-all-start) | async-done | bytes 262176 | tf_op jit(solution)/shard_map/all_to_all | solution.py:41
  18.8 0.1 multiply_reduce_fusion.8
  19.0 3.7 %all_to_all.87 = f32[2,1,64]{2,1,0:T(1,128)S(1)} all-to-all(f32[2,1,64]{2,1,0:T(1,128)S(1)} %broadcast_in_dim.42), channel_id=1, replica_groups=mesh['dp_0'=8,'dp_1'=8,'dp_2'=2,'mp'=4] {'dp_2'}, dimensions={0} | all-to-all | bytes 1024 | tf_op jit(solution)/shard_map/all_to_all | solution.py:41
  22.7 1.3 broadcast_in_dim.41
  23.9 16.6 %all-to-all-start.2 = ((f32[64,1,1]{2,1,0:T(1,128)}), f32[64,1,1]{2,1,0:T(1,128)S(1)}, u32[]{:S(2)}, u32[]{:S(2)}) async-start(f32[64,1,1]{2,1,0:T(1,128)} %broadcast_in_dim.41), calls=%async_computation.2 | async-start | bytes 65536 | tf_op jit(solution)/shard_map/all_to_all | solution.py:41
  40.5 11.0 %all-to-all-done.2 = f32[64,1,1]{2,1,0:T(1,128)S(1)} async-done(((f32[64,1,1]{2,1,0:T(1,128)}), f32[64,1,1]{2,1,0:T(1,128)S(1)}, u32[]{:S(2)}, u32[]{:S(2)}) %all-to-all-start.2) | async-done | bytes 288 | tf_op jit(solution)/shard_map/all_to_all | solution.py:41
  51.5 0.6 broadcast_in_dim.43
  52.1 5.4 %all-to-all-start.4 = ((f32[64,1,64]{2,1,0:T(1,128)}), f32[64,1,64]{2,1,0:T(1,128)S(1)}, u32[]{:S(2)}, u32[]{:S(2)}) async-start(f32[64,1,64]{2,1,0:T(1,128)} %broadcast_in_dim.43), calls=%async_computation.4 | async-start | bytes 65536 | tf_op jit(solution)/shard_map/all_to_all | solution.py:41
  57.6 0.7 reduce_sum.218
  58.3 10.4 %all-to-all-done.4 = f32[64,1,64]{2,1,0:T(1,128)S(1)} async-done(((f32[64,1,64]{2,1,0:T(1,128)}), f32[64,1,64]{2,1,0:T(1,128)S(1)}, u32[]{:S(2)}, u32[]{:S(2)}) %all-to-all-start.4) | async-done | bytes 16416 | tf_op jit(solution)/shard_map/all_to_all | solution.py:41
  68.7 0.6 broadcast_divide_fusion.4
  69.5 0.1 multiply_reduce_fusion.6
  69.6 3.7 %all_to_all.88 = f32[2,1,64]{2,1,0:T(1,128)S(1)} all-to-all(f32[2,1,64]{2,1,0:T(1,128)S(1)} %broadcast_in_dim.44), channel_id=1, replica_groups=mesh['dp_0'=8,'dp_1'=8,'dp_2'=2,'mp'=4] {'dp_2'}, dimensions={0} | all-to-all | bytes 1024 | tf_op jit(solution)/shard_map/all_to_all | solution.py:41
  73.3 15.8 %all_to_all.89 = f32[64,1,64]{2,1,0:T(1,128)S(1)} all-to-all(f32[64,1,64]{2,1,0:T(1,128)S(1)} %broadcast_in_dim.45), channel_id=1, replica_groups=mesh['dp_0'=8,'dp_1'=8,'dp_2'=2,'mp'=4] {'dp_0','dp_1'}, dimensions={0} | all-to-all | bytes 32768 | tf_op jit(solution)/shard_map/all_to_all | solution.py:41
  89.2 0.6 broadcast_divide_fusion.3
  90.0 0.1 multiply_reduce_fusion.4
  90.1 3.7 %all_to_all.90 = f32[2,1,64]{2,1,0:T(1,128)S(1)} all-to-all(f32[2,1,64]{2,1,0:T(1,128)S(1)} %broadcast_in_dim.46), channel_id=1, replica_groups=mesh['dp_0'=8,'dp_1'=8,'dp_2'=2,'mp'=4] {'dp_2'}, dimensions={0} | all-to-all | bytes 1024 | tf_op jit(solution)/shard_map/all_to_all | solution.py:41
  93.8 15.8 %all_to_all.91 = f32[64,1,64]{2,1,0:T(1,128)S(1)} all-to-all(f32[64,1,64]{2,1,0:T(1,128)S(1)} %broadcast_in_dim.47), channel_id=1, replica_groups=mesh['dp_0'=8,'dp_1'=8,'dp_2'=2,'mp'=4] {'dp_0','dp_1'}, dimensions={0} | all-to-all | bytes 32768 | tf_op jit(solution)/shard_map/all_to_all | solution.py:41
  109.7 0.6 broadcast_divide_fusion.2
  110.4 0.1 multiply_reduce_fusion.2
  110.6 3.7 %all_to_all.92 = f32[2,1,64]{2,1,0:T(1,128)S(1)} all-to-all(f32[2,1,64]{2,1,0:T(1,128)S(1)} %broadcast_in_dim.48), channel_id=1, replica_groups=mesh['dp_0'=8,'dp_1'=8,'dp_2'=2,'mp'=4] {'dp_2'}, dimensions={0} | all-to-all | bytes 1024 | tf_op jit(solution)/shard_map/all_to_all | solution.py:41
  114.3 0.6 broadcast_in_dim.49
  114.9 5.6 %all-to-all-start.10 = ((f32[64,1,64]{2,1,0:T(1,128)}), f32[64,1,64]{2,1,0:T(1,128)S(1)}, u32[]{:S(2)}, u32[]{:S(2)}) async-start(f32[64,1,64]{2,1,0:T(1,128)} %broadcast_in_dim.49), calls=%async_computation.10 | async-start | bytes 65536 | tf_op jit(solution)/shard_map/all_to_all | solution.py:41
  120.5 0.7 copy-done.1
  121.2 2.4 %scatter_custom_fusion = bf16[384,1024]{1,0:T(8,128)(2,1)S(1)} fusion(s32[256]{0:T(256)S(1)} %compare_select_fusion, bf16[256,1024]{1,0:T(8,128)(2,1)} %param.5, bf16[]{:T(256)} %constant.14.clone.1), kind=kCustom, calls=%fused_computation.1 | custom fusion | bytes 786944 | tf_op jit(solution)/shard_map/scatter | solution.py:61
  123.6 0.5 reshape_reshape_broadcast_in_dim.3
  124.1 1.5 copy.33
  125.6 6.1 %all-to-all-done.10 = f32[64,1,64]{2,1,0:T(1,128)S(1)} async-done(((f32[64,1,64]{2,1,0:T(1,128)}), f32[64,1,64]{2,1,0:T(1,128)S(1)}, u32[]{:S(2)}, u32[]{:S(2)}) %all-to-all-start.10) | async-done | bytes 16416 | tf_op jit(solution)/shard_map/all_to_all | solution.py:41
  131.7 0.6 broadcast_divide_fusion.1
  132.6 3.7 %all_to_all.93 = f32[2,1,64]{2,1,0:T(1,128)S(1)} all-to-all(f32[2,1,64]{2,1,0:T(1,128)S(1)} %broadcast_in_dim.50), channel_id=1, replica_groups=mesh['dp_0'=8,'dp_1'=8,'dp_2'=2,'mp'=4] {'dp_2'}, dimensions={0} | all-to-all | bytes 1024 | tf_op jit(solution)/shard_map/all_to_all | solution.py:41
  136.3 3.5 %all-to-all-start.13 = ((bf16[64,2,3,1,1024]{4,0,3,2,1:T(8,128)(2,1)}), bf16[64,2,3,1,1024]{4,0,3,2,1:T(8,128)(2,1)S(1)}, u32[]{:S(2)}, u32[]{:S(2)}) async-start(bf16[64,2,3,1,1024]{4,0,3,2,1:T(8,128)(2,1)} %copy.33), calls=%async_computation.13 | async-start | bytes 1572864 | tf_op jit(solution)/shard_map/all_to_all | solution.py:29
  139.9 1.9 all-to-all-done.13
  141.8 0.6 broadcast_in_dim.51
  142.4 6.7 %all-to-all-start.12 = ((f32[64,1,64]{2,1,0:T(1,128)}), f32[64,1,64]{2,1,0:T(1,128)S(1)}, u32[]{:S(2)}, u32[]{:S(2)}) async-start(f32[64,1,64]{2,1,0:T(1,128)} %broadcast_in_dim.51), calls=%async_computation.12 | async-start | bytes 65536 | tf_op jit(solution)/shard_map/all_to_all | solution.py:41
  149.1 1.7 copy.34
  150.8 9.4 %all-to-all-done.12 = f32[64,1,64]{2,1,0:T(1,128)S(1)} async-done(((f32[64,1,64]{2,1,0:T(1,128)}), f32[64,1,64]{2,1,0:T(1,128)S(1)}, u32[]{:S(2)}, u32[]{:S(2)}) %all-to-all-start.12) | async-done | bytes 16416 | tf_op jit(solution)/shard_map/all_to_all | solution.py:41
  160.1 5.5 %all-to-all-start.14 = ((bf16[64,2,3,1,1024]{4,1,3,2,0:T(2,128)(2,1)}), bf16[64,2,3,1,1024]{4,1,3,2,0:T(2,128)(2,1)S(1)}, u32[]{:S(2)}, u32[]{:S(2)}) async-start(bf16[64,2,3,1,1024]{4,1,3,2,0:T(2,128)(2,1)} %copy.34), calls=%async_computation.14 | async-start | bytes 1572864 | tf_op jit(solution)/shard_map/all_to_all | solution.py:29
  165.7 0.6 broadcast_divide_fusion
  166.5 0.6 fusion.5
  167.0 22.7 %all-to-all-done.14 = bf16[64,2,3,1,1024]{4,1,3,2,0:T(2,128)(2,1)S(1)} async-done(((bf16[64,2,3,1,1024]{4,1,3,2,0:T(2,128)(2,1)}), bf16[64,2,3,1,1024]{4,1,3,2,0:T(2,128)(2,1)S(1)}, u32[]{:S(2)}, u32[]{:S(2)}) %all-to-all-start.14) | async-done | bytes 786464 | tf_op jit(solution)/shard_map/all_to_all | solution.py:29
  189.7 0.5 copy.35
  190.3 1.2 reshape.124
  (37 shorter events, 1.0 us)
Async XLA Ops:
  0.6 4.5 %copy-start = (bf16[1024,64]{0,1:T(8,128)(2,1)S(1)}, bf16[1024,64]{0,1:T(8,128)(2,1)}, u32[]{:S(2)}) copy-start(bf16[1024,64]{0,1:T(8,128)(2,1)} %param.6) | copy-start | bytes 393220
  1.9 4.5 %all-to-all-start.1 = ((f32[2,1,1]{2,1,0:T(1,128)}), f32[2,1,1]{2,1,0:T(1,128)S(1)}, u32[]{:S(2)}, u32[]{:S(2)}) async-start(f32[2,1,1]{2,1,0:T(1,128)} %broadcast_in_dim.40), calls=%async_computation.1 | async-start | bytes 2048 | tf_op jit(solution)/shard_map/all_to_all | solution.py:41
  7.2 11.6 %all-to-all-start = ((f32[4,256,64]{1,2,0:T(8,128)}), f32[4,256,64]{1,2,0:T(8,128)S(1)}, u32[]{:S(2)}, u32[]{:S(2)}) async-start(f32[4,256,64]{1,2,0:T(8,128)} %broadcast_in_dim.38), calls=%async_computation | async-start | bytes 524288 | tf_op jit(solution)/shard_map/all_to_all | solution.py:41
  23.9 27.6 %all-to-all-start.2 = ((f32[64,1,1]{2,1,0:T(1,128)}), f32[64,1,1]{2,1,0:T(1,128)S(1)}, u32[]{:S(2)}, u32[]{:S(2)}) async-start(f32[64,1,1]{2,1,0:T(1,128)} %broadcast_in_dim.41), calls=%async_computation.2 | async-start | bytes 65536 | tf_op jit(solution)/shard_map/all_to_all | solution.py:41
  52.1 16.5 %all-to-all-start.4 = ((f32[64,1,64]{2,1,0:T(1,128)}), f32[64,1,64]{2,1,0:T(1,128)S(1)}, u32[]{:S(2)}, u32[]{:S(2)}) async-start(f32[64,1,64]{2,1,0:T(1,128)} %broadcast_in_dim.43), calls=%async_computation.4 | async-start | bytes 65536 | tf_op jit(solution)/shard_map/all_to_all | solution.py:41
  114.9 5.6 %copy-start.2 = (s32[256]{0:T(256)S(1)}, s32[256]{0:T(256)}, u32[]{:S(2)}) copy-start(s32[256]{0:T(256)} %param.9) | copy-start | bytes 3076
  114.9 16.8 %all-to-all-start.10 = ((f32[64,1,64]{2,1,0:T(1,128)}), f32[64,1,64]{2,1,0:T(1,128)S(1)}, u32[]{:S(2)}, u32[]{:S(2)}) async-start(f32[64,1,64]{2,1,0:T(1,128)} %broadcast_in_dim.49), calls=%async_computation.10 | async-start | bytes 65536 | tf_op jit(solution)/shard_map/all_to_all | solution.py:41
  120.5 0.7 copy-start.1
  136.3 5.5 %all-to-all-start.13 = ((bf16[64,2,3,1,1024]{4,0,3,2,1:T(8,128)(2,1)}), bf16[64,2,3,1,1024]{4,0,3,2,1:T(8,128)(2,1)S(1)}, u32[]{:S(2)}, u32[]{:S(2)}) async-start(bf16[64,2,3,1,1024]{4,0,3,2,1:T(8,128)(2,1)} %copy.33), calls=%async_computation.13 | async-start | bytes 1572864 | tf_op jit(solution)/shard_map/all_to_all | solution.py:29
  142.4 17.8 %all-to-all-start.12 = ((f32[64,1,64]{2,1,0:T(1,128)}), f32[64,1,64]{2,1,0:T(1,128)S(1)}, u32[]{:S(2)}, u32[]{:S(2)}) async-start(f32[64,1,64]{2,1,0:T(1,128)} %broadcast_in_dim.51), calls=%async_computation.12 | async-start | bytes 65536 | tf_op jit(solution)/shard_map/all_to_all | solution.py:41
  160.1 29.6 %all-to-all-start.14 = ((bf16[64,2,3,1,1024]{4,1,3,2,0:T(2,128)(2,1)}), bf16[64,2,3,1,1024]{4,1,3,2,0:T(2,128)(2,1)S(1)}, u32[]{:S(2)}, u32[]{:S(2)}) async-start(bf16[64,2,3,1,1024]{4,1,3,2,0:T(2,128)(2,1)} %copy.34), calls=%async_computation.14 | async-start | bytes 1572864 | tf_op jit(solution)/shard_map/all_to_all | solution.py:29
where the time goes:
time: 192 us; the launch traced here: 191 us
  waiting for transfers between devices  68.2 us (36%)
  starting transfers between devices  50.9 us (27%)
  blocking collectives  50.1 us (26%)
  local copies, waits for them, and re-layouts  12.9 us (7%)
  other arithmetic  6.47 us (3%)
    all_to_all x7, blocking collectives, copy_for_each(): lax.all_to_all(jnp.broadcast_to(value[None], (size, *value.shape)), axis,...  50.1 us
    all_to_all x6, waiting for transfers between devices, copy_for_each(): lax.all_to_all(jnp.broadcast_to(value[None], (size, *value.shape)), axis,...  43.6 us
    all_to_all x6, starting transfers between devices, copy_for_each(): lax.all_to_all(jnp.broadcast_to(value[None], (size, *value.shape)), axis,...  41.8 us
    all_to_all x2, waiting for transfers between devices, moved_by_axis(): lax.all_to_all(pieces, axes[k], split_axis=k, concat_axis=k, tiled=True)  24.6 us
    all_to_all x2, starting transfers between devices, moved_by_axis(): lax.all_to_all(pieces, axes[k], split_axis=k, concat_axis=k, tiled=True)  9.05 us
    broadcast_in_dim x13, local copies, waits for them, and re-layouts, copy_for_each(): jnp.broadcast_to(value[None], (size, *value.shape))  4.49 us
  transfers between devices with their start and end apart: 8, of which 7 were waited for; matrix products, arithmetic and copies ran while one was open for 5% of the time, Pallas kernels for 0%

commit v1 on v0

v1 whole, which is shorter than its diff:
```python
import functools

import jax
import jax.numpy as jnp
from jax import lax
from jax.experimental import pallas as pl
from jax.experimental.pallas import tpu as pltpu
from jax.sharding import PartitionSpec as P

E = 64
CAP = 6
ITERS = 5
GROUPS = 128
LINE = 8
XN = 4
ROWS = 256
WIDE = 1024
HELD = 3
META = 128
MESH = pl.DeviceIdType.MESH
NT = (((1,), (1,)), ((), ()))


def f32dot(a, b):
    return jnp.dot(a, b, preferred_element_type=jnp.float32)


def ntdot(a, b):
    return lax.dot_general(a, b, NT, preferred_element_type=jnp.float32)


def split2(x):
    hi = x.astype(jnp.bfloat16)
    lo = (x - hi.astype(jnp.float32)).astype(jnp.bfloat16)
    return hi, lo


def route(
    count_ref, eid_ref, sid_ref, w_ref, tok_hbm,
    gates_ref, land_ref,
    tok_ref, pack_ref, lp_ref, rs_ref, full_ref, gt_ref, gb_ref, mine_ref, ar_ref,
    tok_sem, send_sem, rs_sem, ag_sem, g_sem, ar_sem, d_sem,
):
    dp = lax.axis_index("dp")
    mp = lax.axis_index("mp")
    core = lax.rem(dp, 2)
    y = lax.rem(lax.div(dp, 2), LINE)
    z = lax.div(dp, 2 * LINE)
    mate = dp + 1 - 2 * core

    def x_of(k):
        return lax.rem(mp + k, XN)

    def y_peer(k):
        return z * 16 + lax.rem(y + k, LINE) * 2 + core

    def z_peer(k):
        return lax.rem(z + k, LINE) * 16 + y * 2 + core

    fetch = pltpu.make_async_copy(tok_hbm, tok_ref, tok_sem)
    fetch.start()

    barrier = pltpu.get_barrier_semaphore()
    for k in range(1, XN):
        pl.semaphore_signal(barrier, inc=1, device_id=(dp, x_of(k)), device_id_type=MESH)
        pl.semaphore_signal(barrier, inc=1, device_id=(mate, x_of(k)), device_id_type=MESH)

    @pl.loop(1, GROUPS)
    def _(k):
        pl.semaphore_signal(
            barrier, inc=1, device_id=(lax.rem(dp + k, GROUPS), mp), device_id_type=MESH
        )

    def send(src, dst, ssem, rsem, device):
        pltpu.make_async_remote_copy(
            src_ref=src, dst_ref=dst, send_sem=ssem, recv_sem=rsem,
            device_id=device, device_id_type=MESH,
        ).start()

    def settle(ref, sem):
        pltpu.make_async_copy(ref, ref, sem).wait()

    count = count_ref[0]
    lane = lax.broadcasted_iota(jnp.int32, (128, 128), 1)
    row = lax.broadcasted_iota(jnp.int32, (128, 128), 0)
    low = lane < E
    same = (lane < E) == (row < E)

    target = eid_ref[...] * CAP + sid_ref[...]
    place = lax.broadcasted_iota(jnp.int32, (1, ROWS), 1)
    target = jnp.where(place < count, target, -1)
    slot_row = lax.broadcasted_iota(jnp.int32, (2 * GROUPS, ROWS), 0)
    owner = lax.div(slot_row, 2)
    first = lax.rem(slot_row, 2) == 0
    offset = target - HELD * owner
    at = [jnp.where(offset == s, 1.0, 0.0) for s in range(HELD)]
    used = [jnp.sum(a, axis=1, keepdims=True) for a in at]
    none0 = 1.0 - used[0]
    none01 = none0 * (1.0 - used[1])
    pick0 = at[0] + at[1] * none0 + at[2] * none01
    pick1 = at[1] * (1.0 - none0) + at[2] * (1.0 - none01)
    pick = jnp.where(first, pick0, pick1).astype(jnp.bfloat16)
    code = jnp.broadcast_to(used[0] + 2.0 * used[1] + 4.0 * used[2], (2 * GROUPS, META))

    eid = eid_ref[...].astype(jnp.float32)
    eid_lo = jnp.broadcast_to(eid[:, :128], (128, 128)).T
    eid_hi = jnp.broadcast_to(eid[:, 128:], (128, 128)).T
    chosen = jnp.where(low, eid_lo, eid_hi) == lax.rem(lane, E).astype(jnp.float32)
    live = jnp.where(low, row, row + 128) < count

    fetch.wait()
    la = f32dot(tok_ref[:128, :], w_ref[...])
    lb = f32dot(tok_ref[128:, :], w_ref[...])
    lp_ref[...] = jnp.concatenate([la, lb], axis=1).reshape(XN, 32, 128)

    pl.semaphore_wait(barrier, GROUPS - 1 + 2 * (XN - 1))

    for k in range(1, XN):
        send(lp_ref.at[x_of(k)], rs_ref.at[k - 1], send_sem.at[0], rs_sem, (dp, x_of(k)))

    for j in range(0, WIDE, 256):
        part = f32dot(pick, tok_ref[:, j : j + 256]).astype(jnp.bfloat16)
        pack_ref[:, :, j : j + 256] = part.reshape(GROUPS, 2, 256)
    pack_ref[:, :, WIDE:] = code.astype(jnp.bfloat16).reshape(GROUPS, 2, META)
    land_ref[dp] = pack_ref[dp]

    settle(rs_ref, rs_sem)
    logits = lp_ref[mp] + rs_ref[0] + rs_ref[1] + rs_ref[2]
    full_ref[mp] = logits
    for k in range(1, XN):
        send(full_ref.at[mp], full_ref.at[mp], send_sem.at[1], ag_sem, (dp, x_of(k)))

    qlane = lax.broadcasted_iota(jnp.int32, (32, 128), 1)
    qtok = lax.broadcasted_iota(jnp.int32, (32, 128), 0) + 32 * mp
    qtok = jnp.where(qlane < E, qtok, qtok + 128)
    mixed = lax.rem((dp * ROWS + qtok) * 40503, 65536).astype(jnp.float32)
    dither = 1.0 - mixed * (0.5 / 65536)
    held = jnp.where(qtok < count, jnp.exp(logits) * dither, 0.0).astype(jnp.bfloat16)
    gt_ref[z, y] = held[:16]
    gb_ref[y, z] = held[16:]

    for k in range(1, LINE):
        send(gt_ref.at[z, y], gt_ref.at[z, y], send_sem.at[2], g_sem.at[0], (y_peer(k), mp))
        send(gb_ref.at[y, z], gb_ref.at[y, z], send_sem.at[3], g_sem.at[1], (z_peer(k), mp))
    settle(gt_ref.at[0, pl.ds(0, LINE - 1)], g_sem.at[0])
    for k in range(1, LINE):
        send(gt_ref.at[z], gt_ref.at[z], send_sem.at[4], g_sem.at[2], (z_peer(k), mp))
    settle(gb_ref.at[0, pl.ds(0, LINE - 1)], g_sem.at[1])
    for k in range(1, LINE):
        send(gb_ref.at[y], gb_ref.at[y], send_sem.at[5], g_sem.at[3], (y_peer(k), mp))

    @pl.loop(1, GROUPS)
    def _(k):
        peer = lax.rem(dp + k, GROUPS)
        send(pack_ref.at[peer], land_ref.at[dp], send_sem.at[6], d_sem, (peer, mp))

    settle(gt_ref.at[pl.ds(0, LINE - 1)], g_sem.at[2])
    settle(gb_ref.at[pl.ds(0, LINE - 1)], g_sem.at[3])

    me = mp * 2 + core
    col = jnp.ones((1, 128), jnp.float32)
    before = col
    total = None
    for it in range(ITERS):
        hi, lo = split2(jnp.where(same, jnp.broadcast_to(col, (128, 128)), 0.0))
        acc = jnp.zeros((1, 128), jnp.float32)
        seen = jnp.zeros((1, 128), jnp.float32)
        for ref in (gt_ref, gb_ref):
            for b in range(LINE):
                aff = ref[b].reshape(128, 128)
                rows = ntdot(aff, hi)
                if it > 0:
                    rows = rows + ntdot(aff, lo)
                there = rows > 0.0
                scale = E / jnp.where(there, rows, 1.0)
                acc = acc + jnp.sum(aff.astype(jnp.float32) * scale, axis=0, keepdims=True)
                if it == 0:
                    seen = seen + jnp.sum(jnp.where(there, 1.0, 0.0), axis=0, keepdims=True)
        acc = acc + pltpu.roll(acc, E, 1)
        seen = seen + pltpu.roll(seen, E, 1)
        both = jnp.concatenate([acc, seen], axis=0)
        mine_ref[it] = both
        ar_ref[it, me] = both
        for k in range(XN):
            for other in range(2):
                if k == 0 and other == 0:
                    continue
                device = (mate if other else dp, x_of(k))
                send(mine_ref.at[it], ar_ref.at[it, me], send_sem.at[7], ar_sem.at[it], device)
        settle(ar_ref.at[it, pl.ds(0, 7)], ar_sem.at[it])
        summed = jnp.sum(ar_ref[it], axis=0)
        if it == 0:
            total = summed[1:2]
        before = col
        col = total / summed[0:1]

    settle(full_ref.at[pl.ds(0, XN - 1)], ag_sem)
    aff = jnp.exp(full_ref[...].reshape(128, 128))
    ones = jnp.where(same, 1.0, 0.0).astype(jnp.bfloat16)
    bh, bl = split2(aff * before)
    rows = f32dot(bh, ones) + f32dot(bl, ones)
    gate = jnp.where(chosen & live, aff * col * (E / rows), 0.0)
    srow = lax.broadcasted_iota(jnp.int32, (8, 128), 0)
    slane = lax.broadcasted_iota(jnp.int32, (8, 128), 1)
    side = jnp.where(lax.div(slane, E) == srow, 1.0, 0.0).astype(jnp.bfloat16)
    g1, rest = gate.astype(jnp.bfloat16), None
    rest = gate - g1.astype(jnp.float32)
    g2, g3 = split2(rest)
    out = ntdot(side, g1) + ntdot(side, g2) + ntdot(side, g3)
    gates_ref[...] = out[:2]

    settle(land_ref.at[pl.ds(0, GROUPS - 1)], d_sem)
    settle(rs_ref, send_sem.at[0])
    settle(rs_ref, send_sem.at[1])
    settle(gt_ref.at[0, pl.ds(0, LINE - 1)], send_sem.at[2])
    settle(gt_ref.at[0, pl.ds(0, LINE - 1)], send_sem.at[3])
    settle(gt_ref.at[pl.ds(0, LINE - 1)], send_sem.at[4])
    settle(gt_ref.at[pl.ds(0, LINE - 1)], send_sem.at[5])
    settle(land_ref.at[pl.ds(0, GROUPS - 1)], send_sem.at[6])
    for it in range(ITERS):
        settle(ar_ref.at[it, pl.ds(0, 7)], send_sem.at[7])


def expand(land_ref, gates_ref, out_ref, gout_ref):
    gout_ref[...] = gates_ref[...]
    code = land_ref[:, :, WIDE:].reshape(2 * GROUPS, META).astype(jnp.int32)
    second = lax.rem(lax.broadcasted_iota(jnp.int32, (2 * GROUPS, META), 0), 2)
    bits = [lax.rem(lax.div(code, 2**s), 2) for s in range(HELD)]
    below = [jnp.zeros_like(code), bits[0], bits[0] + bits[1]]
    take = [
        jnp.where((bits[s] == 1) & (below[s] == second), 1.0, 0.0).astype(jnp.bfloat16)
        for s in range(HELD)
    ]
    r = lax.broadcasted_iota(jnp.int32, (GROUPS, 2 * GROUPS), 0)
    c = lax.broadcasted_iota(jnp.int32, (GROUPS, 2 * GROUPS), 1)
    fold = jnp.where(lax.div(c, 2) == r, 1.0, 0.0).astype(jnp.bfloat16)
    for j in range(0, WIDE, 128):
        part = land_ref[:, :, j : j + 128].reshape(2 * GROUPS, 128)
        for s in range(HELD):
            out_ref[s, :, j : j + 128] = f32dot(fold, part * take[s]).astype(jnp.bfloat16)


def local(tokens, router_weight, valid_count, expert_id, slot_id):
    vmem = pl.BlockSpec(memory_space=pltpu.VMEM)
    bf, f32 = jnp.bfloat16, jnp.float32
    gates, land = pl.pallas_call(
        route,
        out_shape=(
            jax.ShapeDtypeStruct((2, 128), f32),
            jax.ShapeDtypeStruct((GROUPS, 2, WIDE + META), bf),
        ),
        in_specs=[
            pl.BlockSpec(memory_space=pltpu.SMEM), vmem, vmem, vmem,
            pl.BlockSpec(memory_space=pl.ANY),
        ],
        out_specs=(vmem, vmem),
        scratch_shapes=[
            pltpu.VMEM((ROWS, WIDE), bf),
            pltpu.VMEM((GROUPS, 2, WIDE + META), bf),
            pltpu.VMEM((XN, 32, 128), f32),
            pltpu.VMEM((XN - 1, 32, 128), f32),
            pltpu.VMEM((XN, 32, 128), f32),
            pltpu.VMEM((LINE, LINE, 16, 128), bf),
            pltpu.VMEM((LINE, LINE, 16, 128), bf),
            pltpu.VMEM((ITERS, 2, 128), f32),
            pltpu.VMEM((ITERS, 8, 2, 128), f32),
            pltpu.SemaphoreType.DMA,
            pltpu.SemaphoreType.DMA((8,)),
            pltpu.SemaphoreType.DMA,
            pltpu.SemaphoreType.DMA,
            pltpu.SemaphoreType.DMA((4,)),
            pltpu.SemaphoreType.DMA((ITERS,)),
            pltpu.SemaphoreType.DMA,
        ],
        compiler_params=pltpu.CompilerParams(collective_id=0, has_side_effects=True),
        name="route",
    )(valid_count, expert_id.reshape(1, ROWS), slot_id.reshape(1, ROWS), router_weight, tokens)
    dispatched, gates = pl.pallas_call(
        expand,
        out_shape=(
            jax.ShapeDtypeStruct((HELD, GROUPS, WIDE), bf),
            jax.ShapeDtypeStruct((2, 128), f32),
        ),
        in_specs=[vmem, vmem],
        out_specs=(vmem, vmem),
        name="expand",
    )(land, gates)
    return gates.reshape(ROWS), dispatched


def solution(mesh):
    return jax.shard_map(
        local,
        mesh=mesh,
        in_specs=(P("dp", "mp"), P("mp", None), P("dp"), P("dp"), P("dp")),
        out_specs=(P("dp"), P("dp", None, "mp")),
        check_vma=False,
    )
```

time: 192 us -> 71.6 us (0.37)
  the two profiles are of different devices: /device:TPU:8 before, /device:TPU:97 now
where the time goes in v1:
time: 71.6 us; the launch traced here: 71.4 us
  Pallas kernels  68.4 us (96%)
  local copies, waits for them, and re-layouts  1.75 us (2%)
  between operations  1.29 us (2%)
    pallas_call x1, Pallas kernels, local(): pl.pallas_call(route, out_shape=(jax.ShapeDtypeStruct((2, 128), f32), jax...  64 us
    pallas_call x1, Pallas kernels, local(): pl.pallas_call(expand, out_shape=(jax.ShapeDtypeStruct((HELD, GROUPS, WID...  4.41 us
    unnamed x1, local copies, waits for them, and re-layouts  1.75 us

profile of v1, /device:TPU:97, one launch (start us, length us, event | category | flops | bytes accessed | tf_op | source)
XLA Modules:
  0.0 71.4 jit_solution(9895374186658875776)
XLA Ops:
  1.3 1.7 %copy.7.w_ref = bf16[1024,64]{1,0:T(8,128)(2,1)} copy(bf16[1024,64]{0,1:T(8,128)(2,1)} %param.6) | data formatting | bytes 262144 | tf_op args[1]
  3.0 64.0 %route.1 = (f32[2,128]{1,0:T(2,128)}, bf16[128,2,1152]{2,1,0:T(2,128)(2,1)}) custom-call(s32[1]{0:T(128)S(6)} %copy.8.count_ref, s32[1,256]{1,0:T(1,128)} %bitcast.3, s32[1,256]{1,0:T(1,128)} %bitcast.4, bf16[1024,64]{1,0:T(8,128)(2,1)} %copy.7.w_ref, bf16[256,1024]{1,0:T(8,128)(2,1)} %tok_hbm.1), custom_call_target="tpu_custom_call" | custom-call | tf_op jit(solution)/shard_map/route/pallas_call | solution.py:246
  67.0 4.4 %expand.1 = (bf16[3,128,1024]{2,1,0:T(8,128)(2,1)}, f32[2,128]{1,0:T(2,128)}) custom-call(bf16[128,2,1152]{2,1,0:T(2,128)(2,1)} %get-tuple-element.6.land_ref, f32[2,128]{1,0:T(2,128)} %get-tuple-element.7.gates_ref), custom_call_target="tpu_custom_call" | custom-call | tf_op jit(solution)/shard_map/expand/pallas_call | solution.py:278

commit v2 on v1

v2 whole, which is shorter than its diff:
```python
import functools

import jax
import jax.numpy as jnp
from jax import lax
from jax.experimental import pallas as pl
from jax.experimental.pallas import tpu as pltpu
from jax.sharding import PartitionSpec as P

E = 64
CAP = 6
ITERS = 5
GROUPS = 128
LINE = 8
SPOTS = 64
XN = 4
ROWS = 256
WIDE = 1024
HELD = 3
META = 128
MESH = pl.DeviceIdType.MESH
NT = (((1,), (1,)), ((), ()))


def f32dot(a, b):
    return jnp.dot(a, b, preferred_element_type=jnp.float32)


def ntdot(a, b):
    return lax.dot_general(a, b, NT, preferred_element_type=jnp.float32)


def split2(x):
    hi = x.astype(jnp.bfloat16)
    lo = (x - hi.astype(jnp.float32)).astype(jnp.bfloat16)
    return hi, lo


def route(
    count_hbm, eid_ref, sid_ref, w_ref, tok_hbm,
    gates_ref, out_hbm,
    held_count, tok_ref, pack_ref, comb_ref, land_ref, lp_ref, rs_ref, full_ref, gt_ref, gb_ref, ar_ref, out_ref,
    count_sem, tok_sem, send_sem, rs_sem, ag_sem, g_sem, ar_sem, m_sem, d_sem, out_sem,
):
    dp = lax.axis_index("dp")
    mp = lax.axis_index("mp")
    core = lax.rem(dp, 2)
    spot = lax.div(dp, 2)
    y = lax.rem(spot, LINE)
    z = lax.div(spot, LINE)
    mate = dp + 1 - 2 * core

    def x_of(k):
        return lax.rem(mp + k, XN)

    def y_peer(k):
        return z * 16 + lax.rem(y + k, LINE) * 2 + core

    def z_peer(k):
        return lax.rem(z + k, LINE) * 16 + y * 2 + core

    fetch = pltpu.make_async_copy(tok_hbm, tok_ref, tok_sem)
    fetch.start()
    counted = pltpu.make_async_copy(count_hbm, held_count, count_sem)
    counted.start()

    barrier = pltpu.get_barrier_semaphore()

    def greet(device):
        pl.semaphore_signal(barrier, inc=1, device_id=device, device_id_type=MESH)

    for k in range(1, LINE):
        greet((y_peer(k), mp))
        greet((z_peer(k), mp))
    greet((mate, mp))
    for k in range(1, XN):
        greet((dp, x_of(k)))
        greet((mate, x_of(k)))

    def send(src, dst, ssem, rsem, device):
        pltpu.make_async_remote_copy(
            src_ref=src, dst_ref=dst, send_sem=ssem, recv_sem=rsem,
            device_id=device, device_id_type=MESH,
        ).start()

    def settle(ref, sem):
        pltpu.make_async_copy(ref, ref, sem).wait()

    fetch.wait()
    whole = ntdot(w_ref[...], tok_ref[...])
    la, lb = whole[:, :128].T, whole[:, 128:].T
    lp_ref[...] = jnp.concatenate([la, lb], axis=1).reshape(XN, 32, 128)

    pl.semaphore_wait(barrier, 2 * (LINE - 1) + 1 + 2 * (XN - 1))

    for k in range(1, XN):
        send(lp_ref.at[x_of(k)], rs_ref.at[k - 1], send_sem.at[0], rs_sem, (dp, x_of(k)))

    lane = lax.broadcasted_iota(jnp.int32, (128, 128), 1)
    row = lax.broadcasted_iota(jnp.int32, (128, 128), 0)
    low = lane < E
    same = (lane < E) == (row < E)

    counted.wait()
    count = held_count[0]
    target = eid_ref[...] * CAP + sid_ref[...]
    place = lax.broadcasted_iota(jnp.int32, (1, ROWS), 1)
    target = jnp.where(place < count, target, -1)
    slot_row = lax.broadcasted_iota(jnp.int32, (2 * GROUPS, ROWS), 0)
    owner = lax.div(lax.rem(slot_row, GROUPS), 2) * 2 + lax.div(slot_row, GROUPS)
    first = lax.rem(slot_row, 2) == 0
    offset = target - HELD * owner
    at = [jnp.where(offset == s, 1.0, 0.0) for s in range(HELD)]
    used = [jnp.sum(a, axis=1, keepdims=True) for a in at]
    none0 = 1.0 - used[0]
    none01 = none0 * (1.0 - used[1])
    pick0 = at[0] + at[1] * none0 + at[2] * none01
    pick1 = at[1] * (1.0 - none0) + at[2] * (1.0 - none01)
    pick = jnp.where(first, pick0, pick1).astype(jnp.bfloat16)
    code = jnp.broadcast_to(used[0] + 2.0 * used[1] + 4.0 * used[2], (2 * GROUPS, META))
    for j in range(0, WIDE, 256):
        part = f32dot(pick, tok_ref[:, j : j + 256]).astype(jnp.bfloat16)
        pack_ref[:, :, :, j : j + 256] = part.reshape(2, SPOTS, 2, 256)
    pack_ref[:, :, :, WIDE:] = code.astype(jnp.bfloat16).reshape(2, SPOTS, 2, META)
    send(pack_ref.at[1 - core], comb_ref.at[core], send_sem.at[6], m_sem, (mate, mp))
    comb_ref[core] = pack_ref[core]

    settle(rs_ref, rs_sem)
    logits = lp_ref[mp] + rs_ref[0] + rs_ref[1] + rs_ref[2]
    full_ref[mp] = logits

    qlane = lax.broadcasted_iota(jnp.int32, (32, 128), 1)
    qtok = lax.broadcasted_iota(jnp.int32, (32, 128), 0) + 32 * mp
    qtok = jnp.where(qlane < E, qtok, qtok + 128)
    mixed = lax.rem((dp * ROWS + qtok) * 40503, 65536).astype(jnp.float32)
    dither = 1.0 - mixed * (0.5 / 65536)
    held = jnp.where(qtok < count, jnp.exp(logits) * dither, 0.0).astype(jnp.bfloat16)
    gt_ref[z, y] = held[:16]
    gb_ref[y, z] = held[16:]

    for k in range(1, LINE):
        send(gt_ref.at[z, y], gt_ref.at[z, y], send_sem.at[2], g_sem.at[0], (y_peer(k), mp))
        send(gb_ref.at[y, z], gb_ref.at[y, z], send_sem.at[3], g_sem.at[1], (z_peer(k), mp))
    for k in range(1, XN):
        send(full_ref.at[mp], full_ref.at[mp], send_sem.at[1], ag_sem, (dp, x_of(k)))

    eid = eid_ref[...].astype(jnp.float32)
    eid_lo = jnp.broadcast_to(eid[:, :128], (128, 128)).T
    eid_hi = jnp.broadcast_to(eid[:, 128:], (128, 128)).T
    chosen = jnp.where(low, eid_lo, eid_hi) == lax.rem(lane, E).astype(jnp.float32)
    chosen = chosen & (jnp.where(low, row, row + 128) < count)

    settle(gt_ref.at[0, pl.ds(0, LINE - 1)], g_sem.at[0])
    for k in range(1, LINE):
        send(gt_ref.at[z], gt_ref.at[z], send_sem.at[4], g_sem.at[2], (z_peer(k), mp))
    settle(gb_ref.at[0, pl.ds(0, LINE - 1)], g_sem.at[1])
    for k in range(1, LINE):
        send(gb_ref.at[y], gb_ref.at[y], send_sem.at[5], g_sem.at[3], (y_peer(k), mp))

    settle(comb_ref.at[0], m_sem)
    for s in range(2):
        land_ref[spot, s] = comb_ref[s, spot]
    settle(gt_ref.at[pl.ds(0, LINE - 1)], g_sem.at[2])
    settle(gb_ref.at[pl.ds(0, LINE - 1)], g_sem.at[3])

    @pl.loop(1, SPOTS)
    def _(k):
        peer = lax.rem(spot + k, SPOTS)
        device = (peer * 2 + core, mp)
        send(comb_ref.at[:, peer], land_ref.at[spot], send_sem.at[7], d_sem, device)

    me = mp * 2 + core
    col = jnp.ones((1, 128), jnp.float32)
    before = col
    total = None
    for it in range(ITERS):
        hi, lo = split2(jnp.where(same, jnp.broadcast_to(col, (128, 128)), 0.0))
        acc = jnp.zeros((1, 128), jnp.float32)
        seen = jnp.zeros((1, 128), jnp.float32)
        for ref in (gt_ref, gb_ref):
            for b in range(LINE):
                aff = ref[b].reshape(128, 128)
                rows = ntdot(aff, hi)
                if it > 0:
                    rows = rows + ntdot(aff, lo)
                there = rows > 0.0
                scale = E / jnp.where(there, rows, 1.0)
                acc = acc + jnp.sum(aff.astype(jnp.float32) * scale, axis=0, keepdims=True)
                if it == 0:
                    seen = seen + jnp.sum(jnp.where(there, 1.0, 0.0), axis=0, keepdims=True)
        acc = acc + pltpu.roll(acc, E, 1)
        seen = seen + pltpu.roll(seen, E, 1)
        ar_ref[it, me] = jnp.concatenate([acc, seen], axis=0)
        for k in range(XN):
            for other in range(2):
                if k == 0 and other == 0:
                    continue
                device = (mate if other else dp, x_of(k))
                send(ar_ref.at[it, me], ar_ref.at[it, me], send_sem.at[8], ar_sem.at[it], device)
        if it == ITERS - 1:
            settle(land_ref.at[pl.ds(0, SPOTS - 1)], d_sem)
            expand(land_ref, out_ref)
            put = pltpu.make_async_copy(out_ref, out_hbm, out_sem)
            put.start()
        settle(ar_ref.at[it, pl.ds(0, 7)], ar_sem.at[it])
        summed = jnp.sum(ar_ref[it], axis=0)
        if it == 0:
            total = summed[1:2]
        before = col
        col = total / summed[0:1]

    settle(full_ref.at[pl.ds(0, XN - 1)], ag_sem)
    aff = jnp.exp(full_ref[...].reshape(128, 128))
    ones = jnp.where(same, 1.0, 0.0).astype(jnp.bfloat16)
    bh, bl = split2(aff * before)
    rows = f32dot(bh, ones) + f32dot(bl, ones)
    gate = jnp.where(chosen, aff * col * (E / rows), 0.0)
    srow = lax.broadcasted_iota(jnp.int32, (8, 128), 0)
    slane = lax.broadcasted_iota(jnp.int32, (8, 128), 1)
    side = jnp.where(lax.div(slane, E) == srow, 1.0, 0.0).astype(jnp.bfloat16)
    g1 = gate.astype(jnp.bfloat16)
    g2, g3 = split2(gate - g1.astype(jnp.float32))
    out = ntdot(side, g1) + ntdot(side, g2) + ntdot(side, g3)
    gates_ref[...] = out[:2]

    put.wait()
    settle(rs_ref, send_sem.at[0])
    settle(rs_ref, send_sem.at[1])
    settle(gt_ref.at[0, pl.ds(0, LINE - 1)], send_sem.at[2])
    settle(gt_ref.at[0, pl.ds(0, LINE - 1)], send_sem.at[3])
    settle(gt_ref.at[pl.ds(0, LINE - 1)], send_sem.at[4])
    settle(gt_ref.at[pl.ds(0, LINE - 1)], send_sem.at[5])
    settle(comb_ref.at[0], send_sem.at[6])
    settle(land_ref.at[pl.ds(0, SPOTS - 1)], send_sem.at[7])
    for it in range(ITERS):
        settle(ar_ref.at[it, pl.ds(0, 7)], send_sem.at[8])


def expand(land_ref, out_ref):
    rows = 2 * GROUPS
    code = land_ref[:, :, :, WIDE:].reshape(rows, META).astype(jnp.int32)
    second = lax.rem(lax.broadcasted_iota(jnp.int32, (rows, META), 0), 2)
    bits = [lax.rem(lax.div(code, 2**s), 2) for s in range(HELD)]
    below = [jnp.zeros_like(code), bits[0], bits[0] + bits[1]]
    take = [
        jnp.where((bits[s] == 1) & (below[s] == second), 1.0, 0.0).astype(jnp.bfloat16)
        for s in range(HELD)
    ]
    r = lax.broadcasted_iota(jnp.int32, (GROUPS, rows), 0)
    c = lax.broadcasted_iota(jnp.int32, (GROUPS, rows), 1)
    fold = jnp.where(lax.div(c, 2) == r, 1.0, 0.0).astype(jnp.bfloat16)
    for j in range(0, WIDE, 128):
        part = land_ref[:, :, :, j : j + 128].reshape(rows, 128)
        for s in range(HELD):
            out_ref[s, :, j : j + 128] = f32dot(fold, part * take[s]).astype(jnp.bfloat16)


def local(tokens, router_weight, valid_count, expert_id, slot_id):
    vmem = pl.BlockSpec(memory_space=pltpu.VMEM)
    anywhere = pl.BlockSpec(memory_space=pl.ANY)
    bf, f32 = jnp.bfloat16, jnp.float32
    gates, dispatched = pl.pallas_call(
        route,
        out_shape=(
            jax.ShapeDtypeStruct((2, 128), f32),
            jax.ShapeDtypeStruct((HELD, GROUPS, WIDE), bf),
        ),
        in_specs=[anywhere, vmem, vmem, vmem, anywhere],
        out_specs=(vmem, anywhere),
        scratch_shapes=[
            pltpu.SMEM((1,), jnp.int32),
            pltpu.VMEM((ROWS, WIDE), bf),
            pltpu.VMEM((2, SPOTS, 2, WIDE + META), bf),
            pltpu.VMEM((2, SPOTS, 2, WIDE + META), bf),
            pltpu.VMEM((SPOTS, 2, 2, WIDE + META), bf),
            pltpu.VMEM((XN, 32, 128), f32),
            pltpu.VMEM((XN - 1, 32, 128), f32),
            pltpu.VMEM((XN, 32, 128), f32),
            pltpu.VMEM((LINE, LINE, 16, 128), bf),
            pltpu.VMEM((LINE, LINE, 16, 128), bf),
            pltpu.VMEM((ITERS, 8, 2, 128), f32),
            pltpu.VMEM((HELD, GROUPS, WIDE), bf),
            pltpu.SemaphoreType.DMA,
            pltpu.SemaphoreType.DMA,
            pltpu.SemaphoreType.DMA((9,)),
            pltpu.SemaphoreType.DMA,
            pltpu.SemaphoreType.DMA,
            pltpu.SemaphoreType.DMA((4,)),
            pltpu.SemaphoreType.DMA((ITERS,)),
            pltpu.SemaphoreType.DMA,
            pltpu.SemaphoreType.DMA,
            pltpu.SemaphoreType.DMA,
        ],
        compiler_params=pltpu.CompilerParams(collective_id=0, has_side_effects=True),
        name="route",
    )(
        valid_count, expert_id.reshape(1, ROWS), slot_id.reshape(1, ROWS),
        router_weight.T, tokens,
    )
    return gates.reshape(ROWS), dispatched


def solution(mesh):
    return jax.shard_map(
        local,
        mesh=mesh,
        in_specs=(P("dp", "mp"), P("mp", None), P("dp"), P("dp"), P("dp")),
        out_specs=(P("dp"), P("dp", None, "mp")),
        check_vma=False,
    )
```

time: 71.6 us -> 59.7 us (0.83)
  the two profiles are of different devices: /device:TPU:97 before, /device:TPU:1 now
where the time goes in v2:
time: 59.7 us; the launch traced here: 59.4 us
  Pallas kernels  54.9 us (92%)
  local copies, waits for them, and re-layouts  3.27 us (5%)
  between operations  1.29 us (2%)
    pallas_call x1, Pallas kernels, local(): pl.pallas_call(route, out_shape=(jax.ShapeDtypeStruct((2, 128), f32), jax...  54.9 us
    unnamed x4, local copies, waits for them, and re-layouts  3.27 us

profile of v2, /device:TPU:1, one launch (start us, length us, event | category | flops | bytes accessed | tf_op | source)
XLA Modules:
  0.0 59.4 jit_solution(1844141694881288604)
XLA Ops:
  1.3 54.9 %route.1 = (f32[2,128]{1,0:T(2,128)}, bf16[3,128,1024]{2,1,0:T(8,128)(2,1)}) custom-call(s32[1]{0:T(128)S(6)} %copy.9.count_hbm, s32[1,256]{1,0:T(1,128)} %bitcast.5, s32[1,256]{1,0:T(1,128)} %bitcast.6, bf16[64,1024]{1,0:T(8,128)(2,1)} %bitcast.4, bf16[256,1024]{1,0:T(8,128)(2,1)} %tok_hbm.1), custom_call_target="tpu_custom_call" | custom-call | tf_op jit(solution)/shard_map/route/pallas_call | solution.py:262
  56.1 0.0 copy-start
  56.2 0.6 %copy-done = f32[2,128]{1,0:T(2,128)S(1)} copy-done((f32[2,128]{1,0:T(2,128)S(1)}, f32[2,128]{1,0:T(2,128)}, u32[]{:S(2)}) %copy-start) | copy-done | bytes 1048
  56.8 0.6 copy.10
  57.4 2.1 %copy.11 = bf16[3,128,1024]{2,1,0:T(8,128)(2,1)} copy(bf16[3,128,1024]{2,1,0:T(8,128)(2,1)} %get-tuple-element.9) | data formatting | bytes 1572864
Async XLA Ops:
  56.1 0.7 %copy-start = (f32[2,128]{1,0:T(2,128)S(1)}, f32[2,128]{1,0:T(2,128)}, u32[]{:S(2)}) copy-start(f32[2,128]{1,0:T(2,128)} %get-tuple-element.4) | copy-start | bytes 3076

commit v3 on v2

--- a/solution.py
+++ b/solution.py
@@ -37,10 +37,11 @@
 
 
 def route(
-    count_hbm, eid_ref, sid_ref, w_ref, tok_hbm,
-    gates_ref, out_hbm,
-    held_count, tok_ref, pack_ref, comb_ref, land_ref, lp_ref, rs_ref, full_ref, gt_ref, gb_ref, ar_ref, out_ref,
-    count_sem, tok_sem, send_sem, rs_sem, ag_sem, g_sem, ar_sem, m_sem, d_sem, out_sem,
+    count_ref, eid_hbm, sid_hbm, w_hbm, tok_hbm,
+    out_ref, full_ref, mask_ref, scale_ref,
+    eid_ref, sid_ref, w_ref, tok_ref,
+    pack_ref, comb_ref, land_ref, lp_ref, rs_ref, gt_ref, gb_ref, ar_ref,
+    in_sem, send_sem, rs_sem, ag_sem, g_sem, ar_sem, m_sem, d_sem,
 ):
     dp = lax.axis_index("dp")
     mp = lax.axis_index("mp")
@@ -59,10 +60,14 @@
     def z_peer(k):
         return lax.rem(z + k, LINE) * 16 + y * 2 + core
 
-    fetch = pltpu.make_async_copy(tok_hbm, tok_ref, tok_sem)
-    fetch.start()
-    counted = pltpu.make_async_copy(count_hbm, held_count, count_sem)
-    counted.start()
+    fetches = [
+        pltpu.make_async_copy(src, dst, in_sem.at[i])
+        for i, (src, dst) in enumerate((
+            (w_hbm, w_ref), (tok_hbm, tok_ref), (eid_hbm, eid_ref), (sid_hbm, sid_ref),
+        ))
+    ]
+    for fetch in fetches:
+        fetch.start()
 
     barrier = pltpu.get_barrier_semaphore()
 
@@ -86,7 +91,8 @@
     def settle(ref, sem):
         pltpu.make_async_copy(ref, ref, sem).wait()
 
-    fetch.wait()
+    fetches[0].wait()
+    fetches[1].wait()
     whole = ntdot(w_ref[...], tok_ref[...])
     la, lb = whole[:, :128].T, whole[:, 128:].T
     lp_ref[...] = jnp.concatenate([la, lb], axis=1).reshape(XN, 32, 128)
@@ -101,8 +107,9 @@
     low = lane < E
     same = (lane < E) == (row < E)
 
-    counted.wait()
-    count = held_count[0]
+    for fetch in fetches[2:]:
+        fetch.wait()
+    count = count_ref[0]
     target = eid_ref[...] * CAP + sid_ref[...]
     place = lax.broadcasted_iota(jnp.int32, (1, ROWS), 1)
     target = jnp.where(place < count, target, -1)
@@ -149,6 +156,7 @@
     eid_hi = jnp.broadcast_to(eid[:, 128:], (128, 128)).T
     chosen = jnp.where(low, eid_lo, eid_hi) == lax.rem(lane, E).astype(jnp.float32)
     chosen = chosen & (jnp.where(low, row, row + 128) < count)
+    mask_ref[...] = jnp.where(chosen, 1.0, 0.0)
 
     settle(gt_ref.at[0, pl.ds(0, LINE - 1)], g_sem.at[0])
     for k in range(1, LINE):
@@ -162,12 +170,6 @@
         land_ref[spot, s] = comb_ref[s, spot]
     settle(gt_ref.at[pl.ds(0, LINE - 1)], g_sem.at[2])
     settle(gb_ref.at[pl.ds(0, LINE - 1)], g_sem.at[3])
-
-    @pl.loop(1, SPOTS)
-    def _(k):
-        peer = lax.rem(spot + k, SPOTS)
-        device = (peer * 2 + core, mp)
-        send(comb_ref.at[:, peer], land_ref.at[spot], send_sem.at[7], d_sem, device)
 
     me = mp * 2 + core
     col = jnp.ones((1, 128), jnp.float32)
@@ -197,11 +199,16 @@
                     continue
                 device = (mate if other else dp, x_of(k))
                 send(ar_ref.at[it, me], ar_ref.at[it, me], send_sem.at[8], ar_sem.at[it], device)
+        if it == 0:
+            @pl.loop(1, SPOTS)
+            def _(k):
+                peer = lax.rem(spot + k, SPOTS)
+                device = (peer * 2 + core, mp)
+                send(comb_ref.at[:, peer], land_ref.at[spot], send_sem.at[7], d_sem, device)
+
         if it == ITERS - 1:
             settle(land_ref.at[pl.ds(0, SPOTS - 1)], d_sem)
             expand(land_ref, out_ref)
-            put = pltpu.make_async_copy(out_ref, out_hbm, out_sem)
-            put.start()
         settle(ar_ref.at[it, pl.ds(0, 7)], ar_sem.at[it])
         summed = jnp.sum(ar_ref[it], axis=0)
         if it == 0:
@@ -209,21 +216,9 @@
         before = col
         col = total / summed[0:1]
 
+    scale_ref[...] = jnp.concatenate([before, col], axis=0)
     settle(full_ref.at[pl.ds(0, XN - 1)], ag_sem)
-    aff = jnp.exp(full_ref[...].reshape(128, 128))
-    ones = jnp.where(same, 1.0, 0.0).astype(jnp.bfloat16)
-    bh, bl = split2(aff * before)
-    rows = f32dot(bh, ones) + f32dot(bl, ones)
-    gate = jnp.where(chosen, aff * col * (E / rows), 0.0)
-    srow = lax.broadcasted_iota(jnp.int32, (8, 128), 0)
-    slane = lax.broadcasted_iota(jnp.int32, (8, 128), 1)
-    side = jnp.where(lax.div(slane, E) == srow, 1.0, 0.0).astype(jnp.bfloat16)
-    g1 = gate.astype(jnp.bfloat16)
-    g2, g3 = split2(gate - g1.astype(jnp.float32))
-    out = ntdot(side, g1) + ntdot(side, g2) + ntdot(side, g3)
-    gates_ref[...] = out[:2]
-
-    put.wait()
+
     settle(rs_ref, send_sem.at[0])
     settle(rs_ref, send_sem.at[1])
     settle(gt_ref.at[0, pl.ds(0, LINE - 1)], send_sem.at[2])
@@ -255,48 +250,82 @@
             out_ref[s, :, j : j + 128] = f32dot(fold, part * take[s]).astype(jnp.bfloat16)
 
 
+def finish(disp_ref, full_ref, mask_ref, scale_ref, out_hbm, gates_hbm, gates_ref, sem):
+    put = pltpu.make_async_copy(disp_ref, out_hbm, sem.at[0])
+    put.start()
+    lane = lax.broadcasted_iota(jnp.int32, (128, 128), 1)
+    row = lax.broadcasted_iota(jnp.int32, (128, 128), 0)
+    aff = jnp.exp(full_ref[...].reshape(128, 128))
+    ones = jnp.where((lane < E) == (row < E), 1.0, 0.0).astype(jnp.bfloat16)
+    bh, bl = split2(aff * scale_ref[0:1])
+    rows = f32dot(bh, ones) + f32dot(bl, ones)
+    gate = jnp.where(mask_ref[...] > 0.0, aff * scale_ref[1:2] * (E / rows), 0.0)
+    srow = lax.broadcasted_iota(jnp.int32, (8, 128), 0)
+    slane = lax.broadcasted_iota(jnp.int32, (8, 128), 1)
+    side = jnp.where(lax.div(slane, E) == srow, 1.0, 0.0).astype(jnp.bfloat16)
+    g1 = gate.astype(jnp.bfloat16)
+    g2, g3 = split2(gate - g1.astype(jnp.float32))
+    out = ntdot(side, g1) + ntdot(side, g2) + ntdot(side, g3)
+    gates_ref[...] = out[:2]
+    gput = pltpu.make_async_copy(gates_ref, gates_hbm, sem.at[1])
+    gput.start()
+    put.wait()
+    gput.wait()
+
+
 def local(tokens, router_weight, valid_count, expert_id, slot_id):
     vmem = pl.BlockSpec(memory_space=pltpu.VMEM)
-    anywhere = pl.BlockSpec(memory_space=pl.ANY)
+    hbm = pl.BlockSpec(memory_space=pltpu.HBM)
     bf, f32 = jnp.bfloat16, jnp.float32
-    gates, dispatched = pl.pallas_call(
+    dma = pltpu.SemaphoreType.DMA
+    parts = pl.pallas_call(
         route,
         out_shape=(
+            jax.ShapeDtypeStruct((HELD, GROUPS, WIDE), bf),
+            jax.ShapeDtypeStruct((XN, 32, 128), f32),
+            jax.ShapeDtypeStruct((128, 128), f32),
             jax.ShapeDtypeStruct((2, 128), f32),
-            jax.ShapeDtypeStruct((HELD, GROUPS, WIDE), bf),
         ),
-        in_specs=[anywhere, vmem, vmem, vmem, anywhere],
-        out_specs=(vmem, anywhere),
+        in_specs=[pl.BlockSpec(memory_space=pltpu.SMEM), *[hbm] * 4],
+        out_specs=(vmem,) * 4,
         scratch_shapes=[
-            pltpu.SMEM((1,), jnp.int32),
+            pltpu.VMEM((1, ROWS), jnp.int32),
+            pltpu.VMEM((1, ROWS), jnp.int32),
+            pltpu.VMEM((E, WIDE), bf),
             pltpu.VMEM((ROWS, WIDE), bf),
             pltpu.VMEM((2, SPOTS, 2, WIDE + META), bf),
             pltpu.VMEM((2, SPOTS, 2, WIDE + META), bf),
             pltpu.VMEM((SPOTS, 2, 2, WIDE + META), bf),
             pltpu.VMEM((XN, 32, 128), f32),
             pltpu.VMEM((XN - 1, 32, 128), f32),
-            pltpu.VMEM((XN, 32, 128), f32),
             pltpu.VMEM((LINE, LINE, 16, 128), bf),
             pltpu.VMEM((LINE, LINE, 16, 128), bf),
             pltpu.VMEM((ITERS, 8, 2, 128), f32),
-            pltpu.VMEM((HELD, GROUPS, WIDE), bf),
-            pltpu.SemaphoreType.DMA,
-            pltpu.SemaphoreType.DMA,
-            pltpu.SemaphoreType.DMA((9,)),
-            pltpu.SemaphoreType.DMA,
-            pltpu.SemaphoreType.DMA,
-            pltpu.SemaphoreType.DMA((4,)),
-            pltpu.SemaphoreType.DMA((ITERS,)),
-            pltpu.SemaphoreType.DMA,
-            pltpu.SemaphoreType.DMA,
-            pltpu.SemaphoreType.DMA,
+            dma((4,)), dma((9,)), dma, dma, dma((4,)), dma((ITERS,)), dma, dma,
         ],
-        compiler_params=pltpu.CompilerParams(collective_id=0, has_side_effects=True),
+        compiler_params=pltpu.CompilerParams(
+            collective_id=0, has_side_effects=True, vmem_limit_bytes=24 * 2**20
+        ),
         name="route",
-    )(
-        valid_count, expert_id.reshape(1, ROWS), slot_id.reshape(1, ROWS),
-        router_weight.T, tokens,
-    )
+    )(valid_count, *(
+        pltpu.with_memory_space_constraint(x, pltpu.HBM)
+        for x in (
+            expert_id.reshape(1, ROWS), slot_id.reshape(1, ROWS),
+            router_weight.T, tokens,
+        )
+    ))
+    dispatched, gates = pl.pallas_call(
+        finish,
+        out_shape=(
+            jax.ShapeDtypeStruct((HELD, GROUPS, WIDE), bf),
+            jax.ShapeDtypeStruct((2, 128), f32),
+        ),
+        in_specs=[vmem] * 4,
+        out_specs=(hbm, hbm),
+        scratch_shapes=[pltpu.VMEM((2, 128), f32), dma((2,))],
+        compiler_params=pltpu.CompilerParams(vmem_limit_bytes=16 * 2**20),
+        name="finish",
+    )(*parts)
     return gates.reshape(ROWS), dispatched
 
 

time: 59.7 us -> 54.6 us (0.915)
  local copies, waits for them, and re-layouts: 3.27 us -> 0 us
  Pallas kernels: 54.9 us -> 53.2 us
    unnamed x4 -> x0, local copies, waits for them, and re-layouts: 3.27 us -> none
    pallas_call x1 -> x2, Pallas kernels: 54.9 us -> 53.2 us  [the longest x1 52.2 us: local(): pl.pallas_call(route, out_shape=(jax.ShapeDtypeStruct((HELD, GROUPS, WIDE...]
where the time goes in v3:
time: 54.6 us; the launch traced here: 54.5 us
  Pallas kernels  53.2 us (97%)
  between operations  1.28 us (2%)
    pallas_call x1, Pallas kernels, local(): pl.pallas_call(route, out_shape=(jax.ShapeDtypeStruct((HELD, GROUPS, WIDE...  52.2 us

profile of v3, /device:TPU:1, one launch (start us, length us, event | category | flops | bytes accessed | tf_op | source)
XLA Modules:
  0.0 54.5 jit_solution(3523276514729008985)
XLA Ops:
  1.3 52.2 %route.1 = (bf16[3,128,1024]{2,1,0:T(8,128)(2,1)S(1)}, f32[4,32,128]{2,1,0:T(8,128)S(1)}, f32[128,128]{1,0:T(8,128)S(1)}, f32[2,128]{1,0:T(2,128)S(1)}) custom-call(s32[1]{0:T(128)S(6)} %copy.7.count_ref, s32[1,256]{1,0:T(1,128)} %bitcast.5, s32[1,256]{1,0:T(1,128)} %bitcast.6, bf16[64,1024]{1,0:T(8,128)(2,1)} %bitcast.4, bf16[256,1024]{1,0:T(8,128)(2,1)} %tok_hbm.1), custom_call_target="tpu_custom_call" | custom-call | tf_op jit(solution)/shard_map/route/pallas_call | solution.py:281
  53.5 0.9 %finish.1 = (bf16[3,128,1024]{2,1,0:T(8,128)(2,1)}, f32[2,128]{1,0:T(2,128)}) custom-call(bf16[3,128,1024]{2,1,0:T(8,128)(2,1)S(1)} %get-tuple-element.8.disp_ref, f32[4,32,128]{2,1,0:T(8,128)S(1)} %get-tuple-element.9.full_ref, f32[128,128]{1,0:T(8,128)S(1)} %get-tuple-element.10.mask_ref, f32[2,128]{1,0:T(2,128)S(1)} %get-tuple-element.11.scale_ref), custom_call_target="tpu_custom_call" | custom-call | tf_op jit(solution)/shard_map/finish/pallas_call | solution.py:317

commit v4 on v3

--- a/solution.py
+++ b/solution.py
@@ -17,6 +17,8 @@
 ROWS = 256
 WIDE = 1024
 HELD = 3
+FAR = (4, 3, 5, 2, 6, 1, 7)
+TINY = 0.9e-37
 META = 128
 MESH = pl.DeviceIdType.MESH
 NT = (((1,), (1,)), ((), ()))
@@ -36,12 +38,18 @@
     return hi, lo
 
 
+def spread(tile):
+    return jnp.concatenate(
+        [jnp.broadcast_to(tile[:, k : k + 1], (8, 128)) for k in range(8)], axis=0
+    )
+
+
 def route(
     count_ref, eid_hbm, sid_hbm, w_hbm, tok_hbm,
-    out_ref, full_ref, mask_ref, scale_ref,
+    out_ref, full_ref, mask_ref, before_ref, last_ref,
     eid_ref, sid_ref, w_ref, tok_ref,
-    pack_ref, comb_ref, land_ref, lp_ref, rs_ref, gt_ref, gb_ref, ar_ref,
-    in_sem, send_sem, rs_sem, ag_sem, g_sem, ar_sem, m_sem, d_sem,
+    pack_ref, comb_ref, land_ref, lp_ref, rs_ref, gt_ref, gb_ref, xsum_ref, ar_ref, ysum_ref, zsum_ref, aff_ref,
+    in_sem, send_sem, rs_sem, ag_sem, g_sem, ar_sem, m_sem, d_sem, c_sem,
 ):
     dp = lax.axis_index("dp")
     mp = lax.axis_index("mp")
@@ -99,7 +107,7 @@
 
     pl.semaphore_wait(barrier, 2 * (LINE - 1) + 1 + 2 * (XN - 1))
 
-    for k in range(1, XN):
+    for k in (2, 1, 3):
         send(lp_ref.at[x_of(k)], rs_ref.at[k - 1], send_sem.at[0], rs_sem, (dp, x_of(k)))
 
     lane = lax.broadcasted_iota(jnp.int32, (128, 128), 1)
@@ -141,14 +149,26 @@
     qtok = jnp.where(qlane < E, qtok, qtok + 128)
     mixed = lax.rem((dp * ROWS + qtok) * 40503, 65536).astype(jnp.float32)
     dither = 1.0 - mixed * (0.5 / 65536)
-    held = jnp.where(qtok < count, jnp.exp(logits) * dither, 0.0).astype(jnp.bfloat16)
+    fresh = jnp.where(qtok < count, jnp.exp(logits) * dither, 0.0)
+    held = fresh.astype(jnp.bfloat16)
     gt_ref[z, y] = held[:16]
     gb_ref[y, z] = held[16:]
 
-    for k in range(1, LINE):
+    for k in FAR:
         send(gt_ref.at[z, y], gt_ref.at[z, y], send_sem.at[2], g_sem.at[0], (y_peer(k), mp))
         send(gb_ref.at[y, z], gb_ref.at[y, z], send_sem.at[3], g_sem.at[1], (z_peer(k), mp))
-    for k in range(1, XN):
+
+    ones = jnp.where(same, 1.0, 0.0).astype(jnp.bfloat16)
+    fh, fl = split2(fresh)
+    rows = f32dot(jnp.concatenate([fh, fl], axis=1), jnp.concatenate([ones, ones], axis=0))
+    there = rows > 0.0
+    acc = jnp.sum(fresh / jnp.where(there, rows, 1.0), axis=0, keepdims=True)
+    seen = jnp.sum(jnp.where(there, 1.0, 0.0), axis=0, keepdims=True)
+    both = jnp.concatenate([acc, seen], axis=0)
+    ysum_ref[y] = both + pltpu.roll(both, E, 1)
+    for k in FAR:
+        send(ysum_ref.at[y], ysum_ref.at[y], send_sem.at[9], c_sem.at[0], (y_peer(k), mp))
+    for k in (2, 1, 3):
         send(full_ref.at[mp], full_ref.at[mp], send_sem.at[1], ag_sem, (dp, x_of(k)))
 
     eid = eid_ref[...].astype(jnp.float32)
@@ -158,65 +178,82 @@
     chosen = chosen & (jnp.where(low, row, row + 128) < count)
     mask_ref[...] = jnp.where(chosen, 1.0, 0.0)
 
+    settle(gb_ref.at[0, pl.ds(0, LINE - 1)], g_sem.at[1])
+    for k in FAR:
+        send(gb_ref.at[y], gb_ref.at[y], send_sem.at[5], g_sem.at[3], (y_peer(k), mp))
+    settle(ysum_ref.at[pl.ds(0, LINE - 1)], c_sem.at[0])
+    zsum_ref[z] = jnp.sum(ysum_ref[...], axis=0)
+    for k in FAR:
+        send(zsum_ref.at[z], zsum_ref.at[z], send_sem.at[9], c_sem.at[1], (z_peer(k), mp))
     settle(gt_ref.at[0, pl.ds(0, LINE - 1)], g_sem.at[0])
-    for k in range(1, LINE):
+    for k in FAR:
         send(gt_ref.at[z], gt_ref.at[z], send_sem.at[4], g_sem.at[2], (z_peer(k), mp))
-    settle(gb_ref.at[0, pl.ds(0, LINE - 1)], g_sem.at[1])
-    for k in range(1, LINE):
-        send(gb_ref.at[y], gb_ref.at[y], send_sem.at[5], g_sem.at[3], (y_peer(k), mp))
 
     settle(comb_ref.at[0], m_sem)
     for s in range(2):
         land_ref[spot, s] = comb_ref[s, spot]
-    settle(gt_ref.at[pl.ds(0, LINE - 1)], g_sem.at[2])
-    settle(gb_ref.at[pl.ds(0, LINE - 1)], g_sem.at[3])
-
     me = mp * 2 + core
-    col = jnp.ones((1, 128), jnp.float32)
-    before = col
-    total = None
-    for it in range(ITERS):
-        hi, lo = split2(jnp.where(same, jnp.broadcast_to(col, (128, 128)), 0.0))
-        acc = jnp.zeros((1, 128), jnp.float32)
-        seen = jnp.zeros((1, 128), jnp.float32)
-        for ref in (gt_ref, gb_ref):
-            for b in range(LINE):
-                aff = ref[b].reshape(128, 128)
-                rows = ntdot(aff, hi)
-                if it > 0:
-                    rows = rows + ntdot(aff, lo)
-                there = rows > 0.0
-                scale = E / jnp.where(there, rows, 1.0)
-                acc = acc + jnp.sum(aff.astype(jnp.float32) * scale, axis=0, keepdims=True)
-                if it == 0:
-                    seen = seen + jnp.sum(jnp.where(there, 1.0, 0.0), axis=0, keepdims=True)
-        acc = acc + pltpu.roll(acc, E, 1)
-        seen = seen + pltpu.roll(seen, E, 1)
-        ar_ref[it, me] = jnp.concatenate([acc, seen], axis=0)
-        for k in range(XN):
-            for other in range(2):
+
+    def share(slots, value, rsem):
+        slots[me] = value
+        for k in (2, 1, 3, 0):
+            for other in (1, 0):
                 if k == 0 and other == 0:
                     continue
                 device = (mate if other else dp, x_of(k))
-                send(ar_ref.at[it, me], ar_ref.at[it, me], send_sem.at[8], ar_sem.at[it], device)
-        if it == 0:
-            @pl.loop(1, SPOTS)
-            def _(k):
-                peer = lax.rem(spot + k, SPOTS)
-                device = (peer * 2 + core, mp)
-                send(comb_ref.at[:, peer], land_ref.at[spot], send_sem.at[7], d_sem, device)
-
-        if it == ITERS - 1:
+                send(slots.at[me], slots.at[me], send_sem.at[8], rsem, device)
+
+    settle(zsum_ref.at[pl.ds(0, LINE - 1)], c_sem.at[1])
+    share(xsum_ref, jnp.sum(zsum_ref[...], axis=0), c_sem.at[2])
+
+    def dispatch(t):
+        def step(i):
+            return 4 + lax.div(i + 1, 2) * (1 - 2 * lax.rem(i, 2))
+
+        pz = lax.rem(z + step(lax.div(t, LINE)), LINE)
+        py = lax.rem(y + step(lax.rem(t, LINE)), LINE)
+        peer = pz * LINE + py
+        device = (peer * 2 + core, mp)
+        send(comb_ref.at[:, peer], land_ref.at[spot], send_sem.at[7], d_sem, device)
+
+    pl.loop(0, SPOTS - 1)(dispatch)
+
+    settle(xsum_ref.at[pl.ds(0, 7)], c_sem.at[2])
+    summed = jnp.sum(xsum_ref[...], axis=0)
+    total = summed[1:2] * (1.0 / E)
+    col = jnp.broadcast_to(total / summed[0:1], (128, 128)).T[:E]
+
+    settle(gb_ref.at[pl.ds(0, LINE - 1)], g_sem.at[3])
+    for b in range(LINE):
+        aff_ref[LINE + b] = gb_ref[b].reshape(128, 128).astype(jnp.float32).T
+    settle(gt_ref.at[pl.ds(0, LINE - 1)], g_sem.at[2])
+    for b in range(LINE):
+        aff_ref[b] = gt_ref[b].reshape(128, 128).astype(jnp.float32).T
+
+    tile_lane = lax.broadcasted_iota(jnp.int32, (8, 128), 1)
+    for it in range(ITERS - 1):
+        acc = jnp.zeros((E, 128), jnp.float32)
+        for b in range(2 * LINE):
+            for half in range(2):
+                aff = aff_ref[b, half * E : half * E + E]
+                rows = jnp.sum(aff * col, axis=0, keepdims=True)
+                acc = acc + aff * (1.0 / jnp.maximum(rows, TINY))
+        acc = jnp.sum(acc, axis=1, keepdims=True)
+        tile = jnp.ones((8, 128), jnp.float32)
+        for k in range(8):
+            tile = jnp.where(tile_lane == k, acc[8 * k : 8 * k + 8], tile)
+        share(ar_ref.at[it], tile, ar_sem.at[it])
+        if it == ITERS - 2:
+            before_ref[...] = jnp.concatenate([col, col], axis=0).T[0:1]
             settle(land_ref.at[pl.ds(0, SPOTS - 1)], d_sem)
             expand(land_ref, out_ref)
         settle(ar_ref.at[it, pl.ds(0, 7)], ar_sem.at[it])
-        summed = jnp.sum(ar_ref[it], axis=0)
-        if it == 0:
-            total = summed[1:2]
-        before = col
-        col = total / summed[0:1]
-
-    scale_ref[...] = jnp.concatenate([before, col], axis=0)
+        tile = total / jnp.sum(ar_ref[it], axis=0)
+        if it < ITERS - 2:
+            col = spread(tile)
+        else:
+            last_ref[...] = tile
+
     settle(full_ref.at[pl.ds(0, XN - 1)], ag_sem)
 
     settle(rs_ref, send_sem.at[0])
@@ -227,7 +264,10 @@
     settle(gt_ref.at[pl.ds(0, LINE - 1)], send_sem.at[5])
     settle(comb_ref.at[0], send_sem.at[6])
     settle(land_ref.at[pl.ds(0, SPOTS - 1)], send_sem.at[7])
-    for it in range(ITERS):
+    for _ in range(2):
+        settle(ysum_ref.at[pl.ds(0, LINE - 1)], send_sem.at[9])
+    settle(xsum_ref.at[pl.ds(0, 7)], send_sem.at[8])
+    for it in range(ITERS - 1):
         settle(ar_ref.at[it, pl.ds(0, 7)], send_sem.at[8])
 
 
@@ -250,16 +290,18 @@
             out_ref[s, :, j : j + 128] = f32dot(fold, part * take[s]).astype(jnp.bfloat16)
 
 
-def finish(disp_ref, full_ref, mask_ref, scale_ref, out_hbm, gates_hbm, gates_ref, sem):
+def finish(disp_ref, full_ref, mask_ref, before_ref, last_ref, out_hbm, gates_hbm, gates_ref, sem):
     put = pltpu.make_async_copy(disp_ref, out_hbm, sem.at[0])
     put.start()
     lane = lax.broadcasted_iota(jnp.int32, (128, 128), 1)
     row = lax.broadcasted_iota(jnp.int32, (128, 128), 0)
     aff = jnp.exp(full_ref[...].reshape(128, 128))
     ones = jnp.where((lane < E) == (row < E), 1.0, 0.0).astype(jnp.bfloat16)
-    bh, bl = split2(aff * scale_ref[0:1])
+    bh, bl = split2(aff * before_ref[...])
     rows = f32dot(bh, ones) + f32dot(bl, ones)
-    gate = jnp.where(mask_ref[...] > 0.0, aff * scale_ref[1:2] * (E / rows), 0.0)
+    last = spread(last_ref[...])
+    last = jnp.concatenate([last, last], axis=0).T[0:1]
+    gate = jnp.where(mask_ref[...] > 0.0, aff * last * (E / rows), 0.0)
     srow = lax.broadcasted_iota(jnp.int32, (8, 128), 0)
     slane = lax.broadcasted_iota(jnp.int32, (8, 128), 1)
     side = jnp.where(lax.div(slane, E) == srow, 1.0, 0.0).astype(jnp.bfloat16)
@@ -284,10 +326,11 @@
             jax.ShapeDtypeStruct((HELD, GROUPS, WIDE), bf),
             jax.ShapeDtypeStruct((XN, 32, 128), f32),
             jax.ShapeDtypeStruct((128, 128), f32),
-            jax.ShapeDtypeStruct((2, 128), f32),
+            jax.ShapeDtypeStruct((1, 128), f32),
+            jax.ShapeDtypeStruct((8, 128), f32),
         ),
         in_specs=[pl.BlockSpec(memory_space=pltpu.SMEM), *[hbm] * 4],
-        out_specs=(vmem,) * 4,
+        out_specs=(vmem,) * 5,
         scratch_shapes=[
             pltpu.VMEM((1, ROWS), jnp.int32),
             pltpu.VMEM((1, ROWS), jnp.int32),
@@ -300,8 +343,12 @@
             pltpu.VMEM((XN - 1, 32, 128), f32),
             pltpu.VMEM((LINE, LINE, 16, 128), bf),
             pltpu.VMEM((LINE, LINE, 16, 128), bf),
-            pltpu.VMEM((ITERS, 8, 2, 128), f32),
-            dma((4,)), dma((9,)), dma, dma, dma((4,)), dma((ITERS,)), dma, dma,
+            pltpu.VMEM((8, 2, 128), f32),
+            pltpu.VMEM((ITERS - 1, 8, 8, 128), f32),
+            pltpu.VMEM((LINE, 2, 128), f32),
+            pltpu.VMEM((LINE, 2, 128), f32),
+            pltpu.VMEM((2 * LINE, 128, 128), f32),
+            dma((4,)), dma((10,)), dma, dma, dma((4,)), dma((ITERS - 1,)), dma, dma, dma((3,)),
         ],
         compiler_params=pltpu.CompilerParams(
             collective_id=0, has_side_effects=True, vmem_limit_bytes=24 * 2**20
@@ -320,7 +367,7 @@
             jax.ShapeDtypeStruct((HELD, GROUPS, WIDE), bf),
             jax.ShapeDtypeStruct((2, 128), f32),
         ),
-        in_specs=[vmem] * 4,
+        in_specs=[vmem] * 5,
         out_specs=(hbm, hbm),
         scratch_shapes=[pltpu.VMEM((2, 128), f32), dma((2,))],
         compiler_params=pltpu.CompilerParams(vmem_limit_bytes=16 * 2**20),

time: 54.6 us -> 59.3 us (1.086)
  Pallas kernels: 53.2 us -> 57.9 us
    pallas_call x1, Pallas kernels: 52.2 us -> 57 us  [local(): pl.pallas_call(route, out_shape=(jax.ShapeDtypeStruct((HELD, GROUPS, WIDE...]
where the time goes in v4:
time: 59.3 us; the launch traced here: 59.2 us
  Pallas kernels  57.9 us (98%)
  between operations  1.28 us (2%)
    pallas_call x1, Pallas kernels, local(): pl.pallas_call(route, out_shape=(jax.ShapeDtypeStruct((HELD, GROUPS, WIDE...  57 us

profile of v4, /device:TPU:1, one launch (start us, length us, event | category | flops | bytes accessed | tf_op | source)
XLA Modules:
  0.0 59.2 jit_solution(16886102649893561785)
XLA Ops:
  1.3 57.0 %route.1 = (bf16[3,128,1024]{2,1,0:T(8,128)(2,1)S(1)}, f32[4,32,128]{2,1,0:T(8,128)S(1)}, f32[128,128]{1,0:T(8,128)S(1)}, f32[1,128]{1,0:T(1,128)S(1)}, f32[8,128]{1,0:T(8,128)S(1)}) custom-call(s32[1]{0:T(128)S(6)} %copy.7.count_ref, s32[1,256]{1,0:T(1,128)} %bitcast.5, s32[1,256]{1,0:T(1,128)} %bitcast.6, bf16[64,1024]{1,0:T(8,128)(2,1)} %bitcast.4, ...), custom_call_target="tpu_custom_call" | custom-call | tf_op jit(solution)/shard_map/route/pallas_call | solution.py:323
  58.3 0.9 %finish.1 = (bf16[3,128,1024]{2,1,0:T(8,128)(2,1)}, f32[2,128]{1,0:T(2,128)}) custom-call(bf16[3,128,1024]{2,1,0:T(8,128)(2,1)S(1)} %get-tuple-element.9.disp_ref, f32[4,32,128]{2,1,0:T(8,128)S(1)} %get-tuple-element.10.full_ref, f32[128,128]{1,0:T(8,128)S(1)} %get-tuple-element.11.mask_ref, f32[1,128]{1,0:T(1,128)S(1)} %get-tuple-element.12.before_ref, ...), custom_call_target="tpu_custom_call" | custom-call | tf_op jit(solution)/shard_map/finish/pallas_call | solution.py:364

commit v5 on v4

--- a/solution.py
+++ b/solution.py
@@ -19,6 +19,7 @@
 HELD = 3
 FAR = (4, 3, 5, 2, 6, 1, 7)
 TINY = 0.9e-37
+AHEAD = 20
 META = 128
 MESH = pl.DeviceIdType.MESH
 NT = (((1,), (1,)), ((), ()))
@@ -49,7 +50,7 @@
     out_ref, full_ref, mask_ref, before_ref, last_ref,
     eid_ref, sid_ref, w_ref, tok_ref,
     pack_ref, comb_ref, land_ref, lp_ref, rs_ref, gt_ref, gb_ref, xsum_ref, ar_ref, ysum_ref, zsum_ref, aff_ref,
-    in_sem, send_sem, rs_sem, ag_sem, g_sem, ar_sem, m_sem, d_sem, c_sem,
+    in_sem, send_sem, rs_sem, ag_sem, g_sem, ar_sem, m_sem, d_sem, c_sem, known_sem,
 ):
     dp = lax.axis_index("dp")
     mp = lax.axis_index("mp")
@@ -109,6 +110,10 @@
 
     for k in (2, 1, 3):
         send(lp_ref.at[x_of(k)], rs_ref.at[k - 1], send_sem.at[0], rs_sem, (dp, x_of(k)))
+    for k in FAR:
+        pl.semaphore_signal(
+            known_sem, inc=1, device_id=(z_peer(k), mp), device_id_type=MESH
+        )
 
     lane = lax.broadcasted_iota(jnp.int32, (128, 128), 1)
     row = lax.broadcasted_iota(jnp.int32, (128, 128), 0)
@@ -171,6 +176,17 @@
     for k in (2, 1, 3):
         send(full_ref.at[mp], full_ref.at[mp], send_sem.at[1], ag_sem, (dp, x_of(k)))
 
+    def dispatch(t):
+        pz = lax.rem(z + lax.div(t, LINE) + lax.rem(t, LINE), LINE)
+        py = lax.rem(y + t, LINE)
+        peer = pz * LINE + py
+        device = (peer * 2 + core, mp)
+        send(comb_ref.at[:, peer], land_ref.at[spot], send_sem.at[7], d_sem, device)
+
+    settle(comb_ref.at[0], m_sem)
+    pl.semaphore_wait(known_sem, LINE - 1)
+    pl.loop(1, 1 + AHEAD)(dispatch)
+
     eid = eid_ref[...].astype(jnp.float32)
     eid_lo = jnp.broadcast_to(eid[:, :128], (128, 128)).T
     eid_hi = jnp.broadcast_to(eid[:, 128:], (128, 128)).T
@@ -189,7 +205,6 @@
     for k in FAR:
         send(gt_ref.at[z], gt_ref.at[z], send_sem.at[4], g_sem.at[2], (z_peer(k), mp))
 
-    settle(comb_ref.at[0], m_sem)
     for s in range(2):
         land_ref[spot, s] = comb_ref[s, spot]
     me = mp * 2 + core
@@ -205,18 +220,6 @@
 
     settle(zsum_ref.at[pl.ds(0, LINE - 1)], c_sem.at[1])
     share(xsum_ref, jnp.sum(zsum_ref[...], axis=0), c_sem.at[2])
-
-    def dispatch(t):
-        def step(i):
-            return 4 + lax.div(i + 1, 2) * (1 - 2 * lax.rem(i, 2))
-
-        pz = lax.rem(z + step(lax.div(t, LINE)), LINE)
-        py = lax.rem(y + step(lax.rem(t, LINE)), LINE)
-        peer = pz * LINE + py
-        device = (peer * 2 + core, mp)
-        send(comb_ref.at[:, peer], land_ref.at[spot], send_sem.at[7], d_sem, device)
-
-    pl.loop(0, SPOTS - 1)(dispatch)
 
     settle(xsum_ref.at[pl.ds(0, 7)], c_sem.at[2])
     summed = jnp.sum(xsum_ref[...], axis=0)
@@ -243,6 +246,8 @@
         for k in range(8):
             tile = jnp.where(tile_lane == k, acc[8 * k : 8 * k + 8], tile)
         share(ar_ref.at[it], tile, ar_sem.at[it])
+        if it == 0:
+            pl.loop(1 + AHEAD, SPOTS)(dispatch)
         if it == ITERS - 2:
             before_ref[...] = jnp.concatenate([col, col], axis=0).T[0:1]
             settle(land_ref.at[pl.ds(0, SPOTS - 1)], d_sem)
@@ -349,6 +354,7 @@
             pltpu.VMEM((LINE, 2, 128), f32),
             pltpu.VMEM((2 * LINE, 128, 128), f32),
             dma((4,)), dma((10,)), dma, dma, dma((4,)), dma((ITERS - 1,)), dma, dma, dma((3,)),
+            pltpu.SemaphoreType.REGULAR,
         ],
         compiler_params=pltpu.CompilerParams(
             collective_id=0, has_side_effects=True, vmem_limit_bytes=24 * 2**20

time: 59.3 us -> 51.4 us (0.87)
  Pallas kernels: 57.9 us -> 49.7 us
    pallas_call x1, Pallas kernels: 57 us -> 48.8 us  [local(): pl.pallas_call(route, out_shape=(jax.ShapeDtypeStruct((HELD, GROUPS, WIDE...]
where the time goes in v5:
time: 51.4 us; the launch traced here: 51 us
  Pallas kernels  49.7 us (97%)
  between operations  1.28 us (2%)
    pallas_call x1, Pallas kernels, local(): pl.pallas_call(route, out_shape=(jax.ShapeDtypeStruct((HELD, GROUPS, WIDE...  48.8 us

profile of v5, /device:TPU:1, one launch (start us, length us, event | category | flops | bytes accessed | tf_op | source)
XLA Modules:
  0.0 51.0 jit_solution(15372341802953606602)
XLA Ops:
  1.3 48.8 %route.1 = (bf16[3,128,1024]{2,1,0:T(8,128)(2,1)S(1)}, f32[4,32,128]{2,1,0:T(8,128)S(1)}, f32[128,128]{1,0:T(8,128)S(1)}, f32[1,128]{1,0:T(1,128)S(1)}, f32[8,128]{1,0:T(8,128)S(1)}) custom-call(s32[1]{0:T(128)S(6)} %copy.7.count_ref, s32[1,256]{1,0:T(1,128)} %bitcast.5, s32[1,256]{1,0:T(1,128)} %bitcast.6, bf16[64,1024]{1,0:T(8,128)(2,1)} %bitcast.4, ...), custom_call_target="tpu_custom_call" | custom-call | tf_op jit(solution)/shard_map/route/pallas_call | solution.py:328
  50.1 0.9 %finish.1 = (bf16[3,128,1024]{2,1,0:T(8,128)(2,1)}, f32[2,128]{1,0:T(2,128)}) custom-call(bf16[3,128,1024]{2,1,0:T(8,128)(2,1)S(1)} %get-tuple-element.9.disp_ref, f32[4,32,128]{2,1,0:T(8,128)S(1)} %get-tuple-element.10.full_ref, f32[128,128]{1,0:T(8,128)S(1)} %get-tuple-element.11.mask_ref, f32[1,128]{1,0:T(1,128)S(1)} %get-tuple-element.12.before_ref, ...), custom_call_target="tpu_custom_call" | custom-call | tf_op jit(solution)/shard_map/finish/pallas_call | solution.py:370

commit v6 on v5

--- a/solution.py
+++ b/solution.py
@@ -20,6 +20,17 @@
 FAR = (4, 3, 5, 2, 6, 1, 7)
 TINY = 0.9e-37
 AHEAD = 20
+
+
+def steps_away(t):
+    return min(t[0], LINE - t[0]) + min(t[1], LINE - t[1])
+
+
+ORDER = sorted(
+    ((a, b) for a in range(LINE) for b in range(LINE) if a + b > 0),
+    key=lambda t: (-steps_away(t), (t[0] + t[1]) % LINE, t),
+)
+ORDER = ORDER[-AHEAD:] + ORDER[:-AHEAD]
 META = 128
 MESH = pl.DeviceIdType.MESH
 NT = (((1,), (1,)), ((), ()))
@@ -177,15 +188,16 @@
         send(full_ref.at[mp], full_ref.at[mp], send_sem.at[1], ag_sem, (dp, x_of(k)))
 
     def dispatch(t):
-        pz = lax.rem(z + lax.div(t, LINE) + lax.rem(t, LINE), LINE)
-        py = lax.rem(y + t, LINE)
+        pz = lax.rem(z + t[0], LINE)
+        py = lax.rem(y + t[1], LINE)
         peer = pz * LINE + py
         device = (peer * 2 + core, mp)
         send(comb_ref.at[:, peer], land_ref.at[spot], send_sem.at[7], d_sem, device)
 
     settle(comb_ref.at[0], m_sem)
     pl.semaphore_wait(known_sem, LINE - 1)
-    pl.loop(1, 1 + AHEAD)(dispatch)
+    for t in ORDER[:AHEAD]:
+        dispatch(t)
 
     eid = eid_ref[...].astype(jnp.float32)
     eid_lo = jnp.broadcast_to(eid[:, :128], (128, 128)).T
@@ -247,7 +259,8 @@
             tile = jnp.where(tile_lane == k, acc[8 * k : 8 * k + 8], tile)
         share(ar_ref.at[it], tile, ar_sem.at[it])
         if it == 0:
-            pl.loop(1 + AHEAD, SPOTS)(dispatch)
+            for t in ORDER[AHEAD:]:
+                dispatch(t)
         if it == ITERS - 2:
             before_ref[...] = jnp.concatenate([col, col], axis=0).T[0:1]
             settle(land_ref.at[pl.ds(0, SPOTS - 1)], d_sem)
@@ -278,21 +291,21 @@
 
 def expand(land_ref, out_ref):
     rows = 2 * GROUPS
-    code = land_ref[:, :, :, WIDE:].reshape(rows, META).astype(jnp.int32)
-    second = lax.rem(lax.broadcasted_iota(jnp.int32, (rows, META), 0), 2)
+    code = land_ref[:, :, :, WIDE:].reshape(rows, META).astype(jnp.float32).T.astype(jnp.int32)
+    r = lax.broadcasted_iota(jnp.int32, (GROUPS, rows), 0)
+    c = lax.broadcasted_iota(jnp.int32, (GROUPS, rows), 1)
+    mine = lax.div(c, 2) == r
+    second = lax.rem(c, 2)
     bits = [lax.rem(lax.div(code, 2**s), 2) for s in range(HELD)]
     below = [jnp.zeros_like(code), bits[0], bits[0] + bits[1]]
     take = [
-        jnp.where((bits[s] == 1) & (below[s] == second), 1.0, 0.0).astype(jnp.bfloat16)
-        for s in range(HELD)
+        jnp.where(mine & (bits[s] == 1) & (below[s] == second), 1.0, 0.0) for s in range(HELD)
     ]
-    r = lax.broadcasted_iota(jnp.int32, (GROUPS, rows), 0)
-    c = lax.broadcasted_iota(jnp.int32, (GROUPS, rows), 1)
-    fold = jnp.where(lax.div(c, 2) == r, 1.0, 0.0).astype(jnp.bfloat16)
-    for j in range(0, WIDE, 128):
-        part = land_ref[:, :, :, j : j + 128].reshape(rows, 128)
-        for s in range(HELD):
-            out_ref[s, :, j : j + 128] = f32dot(fold, part * take[s]).astype(jnp.bfloat16)
+    take = jnp.concatenate(take, axis=0).astype(jnp.bfloat16)
+    for j in range(0, WIDE, 256):
+        part = land_ref[:, :, :, j : j + 256].reshape(rows, 256)
+        out = f32dot(take, part).astype(jnp.bfloat16)
+        out_ref[:, :, j : j + 256] = out.reshape(HELD, GROUPS, 256)
 
 
 def finish(disp_ref, full_ref, mask_ref, before_ref, last_ref, out_hbm, gates_hbm, gates_ref, sem):

time: 51.4 us -> 49.1 us (0.955)
  Pallas kernels: 49.7 us -> 47.6 us
    pallas_call x1, Pallas kernels: 48.8 us -> 46.7 us  [local(): pl.pallas_call(route, out_shape=(jax.ShapeDtypeStruct((HELD, GROUPS, WIDE...]
where the time goes in v6:
time: 49.1 us; the launch traced here: 48.9 us
  Pallas kernels  47.6 us (97%)
  between operations  1.28 us (3%)
    pallas_call x1, Pallas kernels, local(): pl.pallas_call(route, out_shape=(jax.ShapeDtypeStruct((HELD, GROUPS, WIDE...  46.7 us

profile of v6, /device:TPU:1, one launch (start us, length us, event | category | flops | bytes accessed | tf_op | source)
XLA Modules:
  0.0 48.9 jit_solution(9341653933293168011)
XLA Ops:
  1.3 46.7 %route.1 = (bf16[3,128,1024]{2,1,0:T(8,128)(2,1)S(1)}, f32[4,32,128]{2,1,0:T(8,128)S(1)}, f32[128,128]{1,0:T(8,128)S(1)}, f32[1,128]{1,0:T(1,128)S(1)}, f32[8,128]{1,0:T(8,128)S(1)}) custom-call(s32[1]{0:T(128)S(6)} %copy.7.count_ref, s32[1,256]{1,0:T(1,128)} %bitcast.5, s32[1,256]{1,0:T(1,128)} %bitcast.6, bf16[64,1024]{1,0:T(8,128)(2,1)} %bitcast.4, ...), custom_call_target="tpu_custom_call" | custom-call | tf_op jit(solution)/shard_map/route/pallas_call | solution.py:341
  48.0 0.9 %finish.1 = (bf16[3,128,1024]{2,1,0:T(8,128)(2,1)}, f32[2,128]{1,0:T(2,128)}) custom-call(bf16[3,128,1024]{2,1,0:T(8,128)(2,1)S(1)} %get-tuple-element.9.disp_ref, f32[4,32,128]{2,1,0:T(8,128)S(1)} %get-tuple-element.10.full_ref, f32[128,128]{1,0:T(8,128)S(1)} %get-tuple-element.11.mask_ref, f32[1,128]{1,0:T(1,128)S(1)} %get-tuple-element.12.before_ref, ...), custom_call_target="tpu_custom_call" | custom-call | tf_op jit(solution)/shard_map/finish/pallas_call | solution.py:383
